TPU v7x, 32 devices: a whole 2x2x4 slice. The times are simulated.
32 devices in a mesh: gx: 4 (over z), gy: 2 (over y), gz: 4 (over x, core).
Axes of the slice: x: 2, y: 2, z: 4, core: 2. Of those that a mesh axis runs over, the one named last changes fastest.
Arguments:
- coords: float32 [3, 65536], P(None, ('gx', 'gy', 'gz')), may hold values from 0 to 3
- anchor: float32 [3, 65536], P(None, ('gx', 'gy', 'gz')), may hold values from -73 to 76
- atom_types: int32 [65536], P(('gx', 'gy', 'gz')), may hold values from 0 to 63
- halo_send: int32 [27904], P(('gx', 'gy', 'gz')), may hold values from 0 to 2047, as said below
- neighbours: int32 [8192, 8], P(('gx', 'gy', 'gz')), may hold values from 0 to 364, as said below
- live_counts: int32 [8192], P(('gx', 'gy', 'gz')), may hold values from 1 to 8
- rep_coef: float32 [64], replicated, may hold values from 0.5 to 2
- disp_coef: float32 [64], replicated, may hold values from 0.2 to 1
- charge: float32 [64], replicated, may hold values from -1 to 1
- step_history: float32 [8, 3, 65536], P(None, None, ('gx', 'gy', 'gz')), may hold values from -9 to 9
- grad_history: float32 [8, 3, 65536], P(None, None, ('gx', 'gy', 'gz')), may hold values from -72 to 72, as said below
Outputs:
- new_coords: float32 [3, 65536], P(None, ('gx', 'gy', 'gz'))
- energy: float32 [], replicated
Inputs may be any that keep to these rules, and one draw needn't show every extreme that they name: `halo_send`: each of a domain's seven blocks holds distinct local atom indices, rising. `neighbours`: slot 0 of row r is r mod 256, the row's own cluster. `grad_history`: the product of each entry with the matching step_history entry is not negative, and each pair's inner product is positive.
All inputs are finite; a program needn't handle non-finite values.
Results may differ from a plain program's by a relative error of at most 0.0003.
Values sent between devices are 32-bit elements; how exact they have to be, the bound alone decides.
No kernel may reach another device: no remote copies, remote signals or barrier semaphores. Data moves between devices by JAX's collectives and lax.ppermute only.
A program may use at most 64 MiB of HBM per device.

v0:
```python
import functools
import math

import jax
import jax.numpy as jnp
from jax import lax
from jax.experimental import pallas as pl
from jax.experimental.pallas import tpu as pltpu
from jax.sharding import PartitionSpec as P


domain_side = 3.0
step_length = 0.5
AXES = ("gx", "gy", "gz")
f32 = jnp.float32
bf16 = jnp.bfloat16
i32 = jnp.int32


def export_sizes(atoms_local):
    face_rows = atoms_local // 8
    edge_rows = max(atoms_local // 64, 8)
    corner_rows = max(atoms_local // 512, 8)
    return face_rows, edge_rows, corner_rows


def shifted(value, axes, steps):
    shape = [lax.axis_size(axis) for axis in axes]
    pairs = []
    for source in range(math.prod(shape)):
        rest, target, scale = source, 0, 1
        for count in reversed(shape):
            target += (rest % count + steps) % count * scale
            rest //= count
            scale *= count
        pairs.append((source, target))
    return lax.ppermute(value, axes, pairs)


def iota(shape, dim):
    return lax.broadcasted_iota(i32, shape, dim)


def split_parts(value, parts):
    pieces = []
    for part in range(parts):
        piece = value.astype(bf16)
        pieces.append(piece)
        if part + 1 < parts:
            value = value - piece.astype(f32)
    return pieces


def join_parts(stacked, rows, parts):
    total = stacked[(parts - 1) * rows :]
    for part in reversed(range(parts - 1)):
        total = total + stacked[part * rows : (part + 1) * rows]
    return total


def dot_nn(left, right):
    return lax.dot_general(left, right, (((1,), (0,)), ((), ())), preferred_element_type=f32)


def dot_nt(left, right):
    return lax.dot_general(left, right, (((1,), (1,)), ((), ())), preferred_element_type=f32)


def one_hot(condition):
    return jnp.where(condition, 1.0, 0.0).astype(bf16)


def slab_order(sizes):
    face, edge, corner = sizes
    return 3 * face, 3 * edge + corner


def reordered_send(send, sizes):
    face, edge, _ = sizes
    lane = iota(send.shape, 1)
    to_front = pltpu.roll(send, send.shape[1] - edge, 1)
    to_back = pltpu.roll(send, face, 1)
    moved = jnp.where(lane < 3 * face, to_front, to_back)
    return jnp.where((lane >= 2 * face) & (lane < 3 * face + edge), moved, send)


def send_one_hot(send_row, first, rows):
    row = iota((rows, send_row.shape[1]), 0) + first
    return one_hot(row == send_row)


def export_kernel(
    sizes,
    send_hbm, coords_hbm, types_hbm, rep_hbm, disp_hbm, charge_hbm, step_hbm, diff_hbm, anchor_hbm, neigh_hbm, live_hbm,
    pay_z_ref, pay_y_ref, pay_x_ref, pay_e_ref,
    far_z_ref, far_y_ref, far_x_ref,
    par_ref, order_ref,
    coords_ref, step_ref, diff_ref, anchor_ref, neigh_ref, live_ref,
    data_ref, send_pad_ref, send_ref, types_ref, rep_ref, disp_ref, charge_ref, arrived,
):
    face, edge, _ = sizes
    faces, _ = slab_order(sizes)
    pairs = [
        (send_hbm, send_ref), (types_hbm, types_ref), (rep_hbm, rep_ref), (disp_hbm, disp_ref),
        (charge_hbm, charge_ref), (coords_hbm, coords_ref), (step_hbm, step_ref), (diff_hbm, diff_ref),
        (anchor_hbm, anchor_ref), (neigh_hbm, neigh_ref), (live_hbm, live_ref),
    ]
    copies = [pltpu.make_async_copy(source, place, arrived.at[k]) for k, (source, place) in enumerate(pairs)]
    for copy in copies:
        copy.start()
    for copy in copies[:6]:
        copy.wait()
    atoms = coords_ref.shape[1]
    ntypes = rep_ref.shape[1]
    send_pad_ref[...] = jnp.full(send_pad_ref.shape, -1, i32)
    count = send_ref.shape[0]
    for first in range(0, count, 128):
        width = min(128, count - first)
        send_pad_ref[:, first : first + width] = send_ref[pl.ds(first, width)].reshape(1, width)
    send = reordered_send(send_pad_ref[:, : faces + 128], sizes)
    order_ref[:, : faces + 128] = send
    kinds = one_hot(types_ref[...] == iota((ntypes, atoms), 0))
    sub = iota((8, ntypes), 0)
    table = jnp.where(sub == 0, rep_ref[...], jnp.where(sub == 1, disp_ref[...], jnp.where(sub == 2, charge_ref[...], 0.0)))
    table = jnp.concatenate(split_parts(table, 3), axis=0)
    params = join_parts(dot_nn(table, kinds), 8, 3)
    par_ref[...] = params
    data_ref[0:3, :] = coords_ref[...]
    data_ref[3:6, :] = params[0:3]
    data_ref[6:8, :] = params[6:8]
    head = data_ref[...]
    for copy in copies[6:]:
        copy.wait()
    hist = jnp.concatenate([step_ref[...].reshape(-1, atoms), diff_ref[...].reshape(-1, atoms)], axis=0)
    rows = hist.shape[0]
    left = jnp.concatenate(split_parts(head, 3) + split_parts(hist, 2), axis=0)
    total = None
    chunk = 256
    for first in range(0, atoms, chunk):
        part = dot_nn(left[:, first : first + chunk], send_one_hot(send, first, chunk))
        total = part if total is None else total + part
    head = join_parts(total[0:24], 8, 3)
    hist = join_parts(total[24:], rows, 2)
    tail = jnp.concatenate([head[:, faces:], hist[:, faces:], jnp.zeros((8, 128), f32)], axis=0)
    packs = [packed_slab(tail, place, edge) for place in range(4)]
    for place, (ref, pack) in enumerate(((pay_z_ref, 1), (pay_y_ref, 2), (pay_x_ref, None))):
        ref[0:8, :] = head[:, place * face : place * face + 128]
        ref[8:16, :] = head[:, place * face + 128 : (place + 1) * face]
        if pack is not None:
            ref[16:32, :] = packs[pack]
    pay_e_ref[0:16, :] = packs[0]
    pay_e_ref[16:32, :] = packs[3]
    for place, ref in enumerate((far_z_ref, far_y_ref, far_x_ref)):
        ref[...] = hist[:, place * face : (place + 1) * face]


def packed_slab(tail, place, edge):
    group = iota((16, 128), 1) // edge
    packed = jnp.zeros((16, 128), f32)
    for k in range(4):
        turned = pltpu.roll(tail[16 * k : 16 * k + 16], (k - place) % 4 * edge, 1)
        packed = jnp.where(group == k, turned, packed)
    return packed


def spread_rows(rows6, lanes):
    keep = (iota((8, lanes), 1) & 7) == iota((8, lanes), 0)
    return jnp.concatenate(
        [jnp.where(keep, jnp.broadcast_to(row, (8, lanes)), 0.0) for row in rows6], axis=0
    )


def cluster_map(atoms, clusters):
    return one_hot((iota((atoms, clusters), 0) >> 3) == iota((atoms, clusters), 1))


def to_clusters(rows6, lanes, clusters):
    spread = spread_rows(rows6, lanes)
    left = jnp.concatenate(split_parts(spread, 3), axis=0)
    return join_parts(dot_nn(left, cluster_map(lanes, clusters)), spread.shape[0], 3)


def to_atoms(tiles, lanes):
    clusters = tiles.shape[1]
    spread = one_hot((iota((clusters, lanes), 1) >> 3) == iota((clusters, lanes), 0))
    wide = dot_nn(jnp.concatenate(split_parts(tiles, 3), axis=0), spread)
    wide = join_parts(wide, tiles.shape[0], 3)
    keep = (iota((8, lanes), 1) & 7) == iota((8, lanes), 0)
    rows = []
    for comp in range(tiles.shape[0] // 8):
        slab = wide[comp * 8 : (comp + 1) * 8]
        rows.append(jnp.sum(jnp.where(keep, slab, 0.0), axis=0, keepdims=True))
    return rows


def lane_sum(value):
    return jnp.sum(value, axis=1, keepdims=True)


def local_kernel(coords_ref, par_ref, neigh_ref, tiles_ref, other_ref):
    atoms = coords_ref.shape[1]
    clusters = atoms // 8
    slots = neigh_ref.shape[0]
    rows6 = [coords_ref[c : c + 1, :] for c in range(3)] + [par_ref[c : c + 1, :] for c in range(3)]
    tiles = to_clusters(rows6, atoms, clusters)
    tiles_ref[...] = tiles
    left = jnp.concatenate(split_parts(tiles, 3), axis=0)
    rows = tiles.shape[0]
    for slot in range(slots):
        select = one_hot(iota((clusters, clusters), 0) == neigh_ref[slot : slot + 1, :])
        other_ref[:, slot * clusters : (slot + 1) * clusters] = join_parts(dot_nn(left, select), rows, 3)


def gram_kernel(step_ref, diff_ref, gram_ref):
    memory, atoms = step_ref.shape[1:]
    lane = iota((memory, 128), 1)
    sub = iota((memory, 128), 0)
    placed = jnp.zeros((memory, 128), f32)
    for j in range(memory):
        sy = None
        yy = None
        for comp in range(3):
            row = jnp.broadcast_to(diff_ref[comp, j : j + 1, :], (memory, atoms))
            one = step_ref[comp] * row
            two = diff_ref[comp] * row
            sy = one if sy is None else sy + one
            yy = two if yy is None else yy + two
        placed = placed + jnp.where(lane == sub * memory + j, lane_sum(sy), 0.0)
        placed = placed + jnp.where(lane == memory * memory + sub * memory + j, lane_sum(yy), 0.0)
    gram_ref[...] = placed


def merge_kernel(pay_ref, pz_ref, py_ref, pe_ref, out_ref):
    out_ref[0:16, :] = pay_ref[...]
    out_ref[16:32, :] = pz_ref[16:32, :]
    out_ref[32:48, :] = py_ref[16:32, :]
    out_ref[48:64, :] = pe_ref[16:32, :]


def remapped(neigh, clusters, sizes):
    face, edge, _ = (size // 8 for size in sizes)
    edge_first = clusters + 2 * face
    shift = jnp.where(
        neigh >= edge_first + edge + face,
        0,
        jnp.where(neigh >= edge_first + edge, -edge, jnp.where(neigh >= edge_first, face, 0)),
    )
    return neigh + shift


def linear_device(offset):
    total = 0
    for axis, step in zip(AXES, offset):
        count = lax.axis_size(axis)
        total = total * count + (lax.axis_index(axis) + step + count) % count
    return total


def code_bits(code):
    return code // 4, code // 2 % 2, code % 2


def pair_kernel(
    sizes, tiles_ref, other_ref, gram_ref, pz_ref, py_ref, px_ref, pe_ref, neigh_ref, live_ref,
    coords_ref, anchor_ref, step_ref, diff_ref,
    grad_ref, returned_ref, common_ref,
    select_ref, gather_ref, push_ref,
):
    face, edge, _ = sizes
    atoms = coords_ref.shape[1]
    clusters = atoms // 8
    slots = neigh_ref.shape[0]
    faces, edges = slab_order(sizes)
    lanes = faces + 128
    halo_clusters = 128
    memory = step_ref.shape[1]

    group = iota((8, 128), 1) // edge
    tail = jnp.where(
        group == 0,
        pe_ref[0:8, :],
        jnp.where(
            group == 1,
            pltpu.roll(px_ref[16:24, :], edge, 1),
            jnp.where(group == 2, pltpu.roll(px_ref[32:40, :], 2 * edge, 1), pltpu.roll(px_ref[48:56, :], 3 * edge, 1)),
        ),
    )
    halves = [ref[first : first + 8, :] for ref in (pz_ref, py_ref, px_ref) for first in (0, 8)]
    halo = jnp.concatenate(halves + [tail], axis=1)
    lane = iota((1, lanes), 1)
    in_x = (lane >= 2 * face) & ((lane < faces) | (lane >= faces + edge))
    in_y = ((lane >= face) & (lane < 2 * face)) | ((lane >= faces) & (lane < faces + edge)) | (lane >= faces + 2 * edge)
    in_z = (lane < face) | ((lane >= faces) & (lane < faces + 2 * edge)) | (lane >= faces + 3 * edge)
    rows6 = [halo[c : c + 1] for c in range(6)]
    for c, inside in enumerate((in_x, in_y, in_z)):
        rows6[c] = rows6[c] + jnp.where(inside, domain_side, 0.0)
    rows6 = [jnp.where(lane < faces + edges, row, 0.0) for row in rows6]
    halo_tiles = to_clusters(rows6, lanes, halo_clusters)
    left = jnp.concatenate(split_parts(halo_tiles, 3), axis=0)
    rows = halo_tiles.shape[0]

    neigh = remapped(neigh_ref[...], clusters, sizes)
    for slot in range(slots):
        cols = slice(slot * clusters, (slot + 1) * clusters)
        row = neigh[slot : slot + 1, :]
        select_ref[:, cols] = one_hot(iota((clusters + halo_clusters, clusters), 0) == row)
        far = dot_nn(left, select_ref[clusters:, cols])
        gather_ref[:, cols] = other_ref[:, cols] + join_parts(far, rows, 3)

    rank = iota((8, clusters), 0)
    home_id = iota((8, clusters), 1)
    live = jnp.broadcast_to(live_ref[...], (8, clusters))
    full = []
    half = []
    for slot in range(slots):
        on = jnp.where(live > slot, 1.0, 0.0)
        full.append(on)
        half.append(jnp.where(neigh[slot : slot + 1, :] == home_id, 0.0, on))

    energy = jnp.zeros((8, clusters), f32)
    home_rows = [[None] * 8 for _ in range(3)]
    for p in range(8):
        home = [jnp.broadcast_to(tiles_ref[c * 8 + p : c * 8 + p + 1, :], (8, clusters)) for c in range(6)]
        upper = rank > p
        sums = [jnp.zeros((8, clusters), f32) for _ in range(3)]
        for slot in range(slots):
            cols = slice(slot * clusters, (slot + 1) * clusters)
            other = [gather_ref[c * 8 : (c + 1) * 8, cols] for c in range(6)]
            offset = [home[c] - other[c] for c in range(3)]
            dist_sq = offset[0] * offset[0] + offset[1] * offset[1] + offset[2] * offset[2]
            root = lax.rsqrt(1.0 + dist_sq)
            inverse = root * root
            repulse = home[3] * other[3] * inverse
            attract = home[4] * other[4]
            coulomb = home[5] * other[5] * root
            weight = jnp.where(upper, full[slot], half[slot])
            energy = energy + weight * (inverse * (repulse - attract) + coulomb)
            factor = weight * inverse * (inverse * (4.0 * repulse - 2.0 * attract) + coulomb)
            for c in range(3):
                term = factor * offset[c]
                sums[c] = sums[c] + term
                place = (slice(c * 8, (c + 1) * 8), cols)
                push_ref[place] = term if p == 0 else push_ref[place] + term
        for c in range(3):
            home_rows[c][p] = jnp.sum(sums[c], axis=0, keepdims=True)
    home_grad = jnp.concatenate([home_rows[c][p] for c in range(3) for p in range(8)], axis=0)
    back = jnp.concatenate(split_parts(push_ref[...], 2), axis=0)
    tile_grad = join_parts(dot_nt(back, select_ref[...]), 24, 2)
    own = to_atoms(tile_grad[:, :clusters] - home_grad, atoms)
    returned = to_atoms(tile_grad[:, clusters:], lanes)

    step_dots = jnp.zeros((memory, atoms), f32)
    diff_dots = jnp.zeros((memory, atoms), f32)
    moved = jnp.zeros((1, atoms), f32)
    for c in range(3):
        returned_ref[c : c + 1, :] = returned[c]
        displacement = coords_ref[c : c + 1, :] - anchor_ref[c : c + 1, :]
        moved = moved + displacement * displacement
        grad = own[c] + displacement
        grad_ref[c : c + 1, :] = grad
        wide = jnp.broadcast_to(grad, (memory, atoms))
        step_dots = step_dots + step_ref[c] * wide
        diff_dots = diff_dots + diff_ref[c] * wide
    step_sum = lane_sum(step_dots)
    diff_sum = lane_sum(diff_dots)
    energy_sum = lane_sum(jnp.sum(energy, axis=0, keepdims=True)) + 0.5 * lane_sum(moved)
    dots = placed_dots(step_sum, diff_sum)
    dots = dots + jnp.where(iota((1, 128), 1) == 2 * memory, energy_sum, 0.0)
    gram = jnp.sum(gram_ref[...], axis=0, keepdims=True)
    sub8 = iota((8, 128), 0)
    common_ref[...] = jnp.where(sub8 == 6, dots, jnp.where(sub8 == 7, gram, 0.0))


def placed_dots(step_sum, diff_sum):
    memory = step_sum.shape[0]
    sub = iota((memory, 128), 0)
    lane = iota((memory, 128), 1)
    dots = jnp.where(lane == sub, step_sum, 0.0) + jnp.where(lane == sub + memory, diff_sum, 0.0)
    return jnp.sum(dots, axis=0, keepdims=True)


def chunk_kernel(sizes, common_ref, returned_ref, fz_ref, fy_ref, fx_ref, px_ref, pe_ref, chunk_ref):
    face, edge, _ = sizes
    faces, _ = slab_order(sizes)
    rows = fy_ref.shape[0]
    memory = rows // 6
    returned = returned_ref[...]
    far_step = jnp.zeros((memory, face), f32)
    far_diff = jnp.zeros((memory, face), f32)
    for place, hist in enumerate((fz_ref[...], fy_ref[...], fx_ref[...])):
        for c in range(3):
            row = returned[c : c + 1, place * face : (place + 1) * face]
            wide = jnp.broadcast_to(row, (memory, face))
            far_step = far_step + hist[c * memory : (c + 1) * memory] * wide
            far_diff = far_diff + hist[(3 + c) * memory : (4 + c) * memory] * wide
    group = iota((1, 128), 1) // edge
    above_sum = jnp.zeros((memory, 128), f32)
    below_sum = jnp.zeros((memory, 128), f32)
    packs = (pe_ref[0:16, :], px_ref[16:32, :], px_ref[32:48, :], px_ref[48:64, :])
    tails = jnp.concatenate([returned[:, faces:], jnp.zeros((5, 128), f32)], axis=0)
    for place, pack in enumerate(packs):
        turned = [pltpu.roll(tails, (k - place) % 4 * edge, 1) for k in range(4)]
        above = jnp.where(
            group == 1, turned[1][1:2], jnp.where(group == 2, turned[2][0:1], jnp.where(group == 3, turned[3][2:3], 0.0))
        )
        below = jnp.where(
            group == 0, turned[0][0:1], jnp.where(group == 1, turned[1][2:3], jnp.where(group == 2, turned[2][1:2], 0.0))
        )
        above_sum = above_sum + pack[0:8] * jnp.broadcast_to(above, (memory, 128))
        below_sum = below_sum + pack[8:16] * jnp.broadcast_to(below, (memory, 128))
    both = above_sum + below_sum
    step_sum = lane_sum(far_step) + lane_sum(jnp.where(group < 2, both, 0.0))
    diff_sum = lane_sum(far_diff) + lane_sum(jnp.where(group < 2, 0.0, both))
    common = common_ref[...] + jnp.where(iota((8, 128), 0) == 6, placed_dots(step_sum, diff_sum), 0.0)
    for device in range(chunk_ref.shape[0]):
        chunk_ref[device] = common
    for code in range(1, 8):
        target = linear_device(code_bits(code))
        start = {1: 0, 2: face, 4: 2 * face}.get(code, faces)
        pieces = [returned[:, start : start + 128]]
        if code in (1, 2, 4):
            pieces.append(returned[:, start + 128 : start + 256])
        chunk_ref[target, 0 : 3 * len(pieces), :] = jnp.concatenate(pieces, axis=0)


def finish_kernel(sizes, atoms_total, recv_ref, send_ref, grad_ref, coords_ref, step_ref, diff_ref, new_ref, energy_ref):
    _, edge, _ = sizes
    faces, edges = slab_order(sizes)
    atoms = coords_ref.shape[1]
    memory = step_ref.shape[1]
    devices = recv_ref.shape[0]
    total = recv_ref[0]
    for device in range(1, devices):
        total = total + recv_ref[device]
    dots = jnp.broadcast_to(total[6:7, :], (memory, 128))
    gram = jnp.broadcast_to(total[7:8, :], (memory, 128))
    sub = iota((memory, 128), 0)
    lane = iota((memory, 128), 1)

    def pick(row, where):
        return jnp.broadcast_to(lane_sum(jnp.where(where, row, 0.0)), (memory, 128))

    def at(value, m):
        return jnp.broadcast_to(value[m : m + 1, :], (memory, 128))

    step_dots = pick(dots, lane == sub)
    diff_dots = pick(dots, lane == sub + memory)
    energy_ref[...] = lane_sum(jnp.where(iota((1, 128), 1) == 2 * memory, total[6:7, :], 0.0)) / atoms_total
    sy_col = [pick(gram, lane == sub * memory + j) for j in range(memory)]
    sy_row = [pick(gram, lane == j * memory + sub) for j in range(memory)]
    yy_col = [pick(gram, lane == memory * memory + sub * memory + j) for j in range(memory)]
    diagonal = pick(gram, lane == sub * (memory + 1))
    rho = 1.0 / diagonal
    last = memory - 1
    scaling = at(diagonal, last) / at(yy_col[last], last)
    left = step_dots
    alpha = jnp.zeros((memory, 128), f32)
    folded = diff_dots
    for m in reversed(range(memory)):
        value = at(left * rho, m)
        alpha = jnp.where(sub == m, value, alpha)
        left = left - value * sy_col[m]
        folded = folded - value * yy_col[m]
    left = diagonal * alpha - scaling * folded
    coef = jnp.zeros((memory, 128), f32)
    for m in range(memory):
        value = at(left * rho, m)
        coef = jnp.where(sub == m, value, coef)
        left = left - value * sy_row[m]
    diff_coef = -scaling * alpha

    blocks = {code: recv_ref[linear_device(tuple(-bit for bit in code_bits(code)))] for code in range(1, 8)}
    edge_lane = iota((8, 128), 1)
    tail = jnp.where(
        edge_lane < edge,
        blocks[3],
        jnp.where(edge_lane < 2 * edge, blocks[5], jnp.where(edge_lane < 3 * edge, blocks[6], blocks[7])),
    )
    tail = jnp.where(edge_lane < edges, tail, 0.0)
    pieces = []
    for code in (1, 2, 4):
        pieces += [blocks[code][0:3], blocks[code][3:6]]
    pieces.append(tail[0:3])
    returned = jnp.concatenate([jnp.concatenate(pieces, axis=1), jnp.zeros((5, faces + 128), f32)], axis=0)
    back = jnp.concatenate(split_parts(returned, 2), axis=0)
    send = send_ref[:, : faces + 128]
    added = []
    chunk = 256
    for first in range(0, atoms, chunk):
        added.append(join_parts(dot_nt(back, send_one_hot(send, first, chunk)), 8, 2))
    added = jnp.concatenate(added, axis=1)
    widen = atoms // 128
    for c in range(3):
        grad = grad_ref[c : c + 1, :] + added[c : c + 1, :]
        mixed = jnp.tile(coef, (1, widen)) * step_ref[c] + jnp.tile(diff_coef, (1, widen)) * diff_ref[c]
        direction = jnp.tile(scaling[0:1], (1, widen)) * grad + jnp.sum(mixed, axis=0, keepdims=True)
        new_ref[c : c + 1, :] = coords_ref[c : c + 1, :] - step_length * direction


def call(kernel, outs, scratch, *args, limit_mib=16, space=pltpu.VMEM):
    if space == pltpu.HBM:
        args = [pltpu.with_memory_space_constraint(arg, pltpu.HBM) for arg in args]
    return pl.pallas_call(
        kernel,
        out_shape=[jax.ShapeDtypeStruct(shape, dtype) for shape, dtype in outs],
        in_specs=[pl.BlockSpec(memory_space=space)] * len(args),
        out_specs=[pl.BlockSpec(memory_space=pltpu.VMEM)] * len(outs),
        scratch_shapes=scratch,
        compiler_params=pltpu.CompilerParams(vmem_limit_bytes=limit_mib << 20),
    )(*args)


def on_device(
    coords,
    anchor,
    atom_types,
    halo_send,
    neighbours,
    live_counts,
    rep_coef,
    disp_coef,
    charge,
    step_history,
    grad_history,
):
    atoms = coords.shape[1]
    clusters = atoms // 8
    memory = step_history.shape[0]
    sizes = export_sizes(atoms)
    face, edge, corner = sizes
    faces, _ = slab_order(sizes)
    lanes = faces + 128
    wide = pl.cdiv(lanes, 1024) * 1024
    slots = neighbours.shape[1]
    devices = lax.axis_size("gx") * lax.axis_size("gy") * lax.axis_size("gz")
    assert edge == 32 and corner <= edge and face == 256 and memory == 8
    steps = step_history.transpose(1, 0, 2)
    diffs = grad_history.transpose(1, 0, 2)
    neigh = neighbours.T
    live = live_counts[None]
    rows = 6 * memory

    ntypes = rep_coef.shape[0]
    pay_z, pay_y, pay_x, pay_e, far_z, far_y, far_x, params, order, coords_v, steps_v, diffs_v, anchor_v, neigh_v, live_v = call(
        functools.partial(export_kernel, sizes),
        [((32, 128), f32)] * 2
        + [((16, 128), f32), ((32, 128), f32)]
        + [((rows, face), f32)] * 3
        + [((8, atoms), f32), ((1, wide), i32)]
        + [(value.shape, value.dtype) for value in (coords, steps, diffs, anchor, neigh, live)],
        [
            pltpu.VMEM((8, atoms), f32),
            pltpu.VMEM((1, wide), i32),
            pltpu.VMEM(halo_send.shape, i32),
            pltpu.VMEM((1, atoms), i32),
            pltpu.VMEM((1, ntypes), f32),
            pltpu.VMEM((1, ntypes), f32),
            pltpu.VMEM((1, ntypes), f32),
            pltpu.SemaphoreType.DMA((11,)),
        ],
        halo_send, coords, atom_types[None], rep_coef[None], disp_coef[None], charge[None],
        steps, diffs, anchor, neigh, live,
        space=pltpu.HBM,
    )
    pe = shifted(pay_e, ("gy", "gz"), -1)
    py = shifted(pay_y, ("gy",), -1)
    pz = shifted(pay_z, ("gz",), -1)
    fx = shifted(far_x, ("gx",), -1)
    fy = shifted(far_y, ("gy",), -1)
    fz = shifted(far_z, ("gz",), -1)
    tiles, other = call(
        local_kernel,
        [((48, clusters), f32), ((48, slots * clusters), f32)],
        [],
        coords_v, params, neigh_v,
    )
    (pay_x,) = call(merge_kernel, [((64, 128), f32)], [], pay_x, pz, py, pe, limit_mib=4)
    px = shifted(pay_x, ("gx",), -1)
    (gram,) = call(gram_kernel, [((memory, 128), f32)], [], steps_v, diffs_v, limit_mib=8)
    grad, returned, common = call(
        functools.partial(pair_kernel, sizes),
        [((3, atoms), f32), ((3, lanes), f32), ((8, 128), f32)],
        [
            pltpu.VMEM((clusters + 128, slots * clusters), bf16),
            pltpu.VMEM((48, slots * clusters), f32),
            pltpu.VMEM((24, slots * clusters), f32),
        ],
        tiles, other, gram, pz, py, px, pe, neigh_v, live_v, coords_v, anchor_v, steps_v, diffs_v,
        limit_mib=24,
    )
    (chunks,) = call(
        functools.partial(chunk_kernel, sizes),
        [((devices, 8, 128), f32)],
        [],
        common, returned, fz, fy, fx, px, pe,
        limit_mib=24,
    )
    received = lax.all_to_all(chunks, AXES, 0, 0, tiled=True)
    new_coords, energy = call(
        functools.partial(finish_kernel, sizes, atoms * devices),
        [((3, atoms), f32), ((1, 1), f32)],
        [],
        received, order, grad, coords_v, steps_v, diffs_v,
    )
    return (new_coords, energy[0, 0])


def solution(mesh):
    placed = (
        P(None, AXES),
        P(None, AXES),
        P(AXES),
        P(AXES),
        P(AXES, None),
        P(AXES),
        P(),
        P(),
        P(),
        P(None, None, AXES),
        P(None, None, AXES),
    )

    return jax.shard_map(
        on_device,
        mesh=mesh,
        in_specs=placed,
        out_specs=(P(None, AXES), P()),
        check_vma=False,
    )
```

profile of v0, /device:TPU:0, one launch (start us, length us, event | category | flops | bytes accessed | tf_op | source)
XLA Modules:
  0.0 32.6 jit_solution(18029900790651439523)
XLA Ops:
  0.6 2.1 %shard_map.122 = (f32[32,128]{1,0:T(8,128)S(1)}, f32[32,128]{1,0:T(8,128)S(1)}, f32[16,128]{1,0:T(8,128)S(1)}, f32[32,128]{1,0:T(8,128)S(1)}, f32[48,256]{1,0:T(...) custom-call(s32[872]{0:T(1024)} %send_hbm.1, ...), custom_call_target="tpu_custom_call" | custom-call | tf_op jit(solution)/shard_map/pallas_call | solution.py:503
  2.7 2.5 %collective-permute-start = (f32[32,128]{1,0:T(8,128)S(1)}, f32[32,128]{1,0:T(8,128)S(1)}, u32[]{:S(2)}, u32[]{:S(2)}) collective-permute-start(f32[32,128]{1,0:T(8,128)S(1)} %get-tuple-element.31), channel_id=1, source_target_pairs={{0,3},{1,0},{2,1},{3,2},{4,7},{5,4},{6,5},{7,6},{8,11},{9,8},{10,9... | collective-permute-start | bytes 49160 | tf_op jit(solution)/shard_map/ppermute | solution.py:37
  5.2 1.5 %collective-permute-start.1 = (f32[32,128]{1,0:T(8,128)S(1)}, f32[32,128]{1,0:T(8,128)S(1)}, u32[]{:S(2)}, u32[]{:S(2)}) collective-permute-start(f32[32,128]{1,0:T(8,128)S(1)} %get-tuple-element.32), channel_id=1, source_target_pairs={{0,4},{4,0},{1,5},{5,1},{2,6},{6,2},{3,7},{7,3},{8,12},{12,8},{9,1... | collective-permute-start | bytes 49160 | tf_op jit(solution)/shard_map/ppermute | solution.py:37
  6.7 0.3 %collective-permute-start.2 = (f32[32,128]{1,0:T(8,128)S(1)}, f32[32,128]{1,0:T(8,128)S(1)}, u32[]{:S(2)}, u32[]{:S(2)}) collective-permute-start(f32[32,128]{1,0:T(8,128)S(1)} %get-tuple-element.34), channel_id=1, source_target_pairs={{0,7},{1,4},{2,5},{3,6},{4,3},{5,0},{6,1},{7,2},{8,15},{9,12},{10,... | collective-permute-start | bytes 49160 | tf_op jit(solution)/shard_map/ppermute | solution.py:37
  7.0 0.5 %collective-permute-start.4 = (f32[48,256]{1,0:T(8,128)S(1)}, f32[48,256]{1,0:T(8,128)S(1)}, u32[]{:S(2)}, u32[]{:S(2)}) collective-permute-start(f32[48,256]{1,0:T(8,128)S(1)} %get-tuple-element.39), channel_id=1, source_target_pairs={{0,3},{1,0},{2,1},{3,2},{4,7},{5,4},{6,5},{7,6},{8,11},{9,8},{10,9... | collective-permute-start | bytes 147464 | tf_op jit(solution)/shard_map/ppermute | solution.py:37
  7.6 1.5 %collective-permute-start.5 = (f32[48,256]{1,0:T(8,128)S(1)}, f32[48,256]{1,0:T(8,128)S(1)}, u32[]{:S(2)}, u32[]{:S(2)}) collective-permute-start(f32[48,256]{1,0:T(8,128)S(1)} %get-tuple-element.40), channel_id=1, source_target_pairs={{0,4},{4,0},{1,5},{5,1},{2,6},{6,2},{3,7},{7,3},{8,12},{12,8},{9,1... | collective-permute-start | bytes 147464 | tf_op jit(solution)/shard_map/ppermute | solution.py:37
  9.1 0.0 collective-permute-done.pz_ref
  9.1 3.6 %collective-permute-start.6 = (f32[48,256]{1,0:T(8,128)S(1)}, f32[48,256]{1,0:T(8,128)S(1)}, u32[]{:S(2)}, u32[]{:S(2)}) collective-permute-start(f32[48,256]{1,0:T(8,128)S(1)} %get-tuple-element.41), channel_id=1, source_target_pairs={{0,24},{8,0},{16,8},{24,16},{1,25},{9,1},{17,9},{25,17},{2,26},{10... | collective-permute-start | bytes 147464 | tf_op jit(solution)/shard_map/ppermute | solution.py:37
  12.7 0.0 collective-permute-done.1.py_ref
  12.7 0.0 collective-permute-done.2.pe_ref
  12.7 0.8 %collective-permute-start.3 = (f32[64,128]{1,0:T(8,128)S(1)}, f32[64,128]{1,0:T(8,128)S(1)}, u32[]{:S(2)}, u32[]{:S(2)}) collective-permute-start(f32[64,128]{1,0:T(8,128)S(1)} %shard_map.125), channel_id=1, source_target_pairs={{0,24},{8,0},{16,8},{24,16},{1,25},{9,1},{17,9},{25,17},{2,26},{10... | collective-permute-start | bytes 98312 | tf_op jit(solution)/shard_map/ppermute | solution.py:37
  13.5 0.4 %shard_map.124.gram_ref = f32[8,128]{1,0:T(8,128)S(1)} custom-call(f32[3,8,2048]{2,1,0:T(8,128)S(1)} %get-tuple-element.29.step_ref, f32[3,8,2048]{2,1,0:T(8,128)S(1)} %get-tuple-element.30.diff_ref), custom_call_target="tpu_custom_call" | custom-call | tf_op jit(solution)/shard_map/pallas_call | solution.py:503
  13.9 0.9 %shard_map.123 = (f32[48,256]{1,0:T(8,128)S(1)}, f32[48,2048]{1,0:T(8,128)S(1)}) custom-call(f32[3,2048]{1,0:T(4,128)S(1)} %get-tuple-element.24.coords_ref, f32[8,2048]{1,0:T(8,128)S(1)} %get-tuple-element.25.par_ref, s32[8,256]{1,0:T(8,128)S(1)} %get-tuple-element.26.neigh_ref), custom_call_target="tpu_custom_call" | custom-call | tf_op jit(solution)/shard_map/pallas_call | solution.py:503
  14.7 1.9 %collective-permute-done.3.px_ref = f32[64,128]{1,0:T(8,128)S(1)} collective-permute-done((f32[64,128]{1,0:T(8,128)S(1)}, f32[64,128]{1,0:T(8,128)S(1)}, u32[]{:S(2)}, u32[]{:S(2)}) %collective-permute-start.3) | collective-permute-done | bytes 32800 | tf_op jit(solution)/shard_map/ppermute | solution.py:37
  16.7 2.2 %shard_map.126 = (f32[3,2048]{1,0:T(4,128)S(1)}, f32[3,896]{1,0:T(4,128)S(1)}, f32[8,128]{1,0:T(8,128)S(1)}) custom-call(f32[48,256]{1,0:T(8,128)S(1)} %get-tuple-element.27.tiles_ref, f32[48,2048]{1,0:T(8,128)S(1)} %get-tuple-element.28.other_ref, f32[8,128]{1,0:T(8,128)S(1)} %shard_map.124.gram_ref, f32[32,128]{1,0:T(8,128)S(1)} %collective-permute-done.pz_ref, ...), custom_call_target="tpu_custom_call" | custom-call | tf_op jit(solution)/shard_map/pallas_call | solution.py:503
  18.8 0.0 collective-permute-done.4.fz_ref
  18.8 0.0 collective-permute-done.5.fy_ref
  18.8 0.0 collective-permute-done.6.fx_ref
  18.9 0.2 shard_map.127
  19.0 11.8 %all_to_all.5.recv_ref = f32[32,8,128]{2,1,0:T(8,128)S(1)} all-to-all(f32[32,8,128]{2,1,0:T(8,128)S(1)} %shard_map.127), channel_id=1, replica_groups=mesh['gx'=4,'gy'=2,'gz'=4] {'gx','gy','gz'}, dimensions={0} | all-to-all | bytes 262144 | tf_op jit(solution)/shard_map/all_to_all | solution.py:598
  30.8 1.7 %shard_map.128 = (f32[3,2048]{1,0:T(4,128)}, f32[1,1]{1,0:T(1,128)}) custom-call(f32[32,8,128]{2,1,0:T(8,128)S(1)} %all_to_all.5.recv_ref, s32[1,1024]{1,0:T(1,128)S(1)} %get-tuple-element.42.send_ref, f32[3,2048]{1,0:T(4,128)S(1)} %get-tuple-element.43.grad_ref, f32[3,2048]{1,0:T(4,128)S(1)} %get-tuple-element.24.coords_ref, ...), custom_call_target="tpu_custom_call" | custom-call | tf_op jit(solution)/shard_map/pallas_call | solution.py:503
  (1 shorter events, 0.0 us)
Async XLA Ops:
  2.7 6.4 %collective-permute-start = (f32[32,128]{1,0:T(8,128)S(1)}, f32[32,128]{1,0:T(8,128)S(1)}, u32[]{:S(2)}, u32[]{:S(2)}) collective-permute-start(f32[32,128]{1,0:T(8,128)S(1)} %get-tuple-element.31), channel_id=1, source_target_pairs={{0,3},{1,0},{2,1},{3,2},{4,7},{5,4},{6,5},{7,6},{8,11},{9,8},{10,9... | collective-permute-start | bytes 49160 | tf_op jit(solution)/shard_map/ppermute | solution.py:37
  5.2 7.5 %collective-permute-start.1 = (f32[32,128]{1,0:T(8,128)S(1)}, f32[32,128]{1,0:T(8,128)S(1)}, u32[]{:S(2)}, u32[]{:S(2)}) collective-permute-start(f32[32,128]{1,0:T(8,128)S(1)} %get-tuple-element.32), channel_id=1, source_target_pairs={{0,4},{4,0},{1,5},{5,1},{2,6},{6,2},{3,7},{7,3},{8,12},{12,8},{9,1... | collective-permute-start | bytes 49160 | tf_op jit(solution)/shard_map/ppermute | solution.py:37
  6.7 6.0 %collective-permute-start.2 = (f32[32,128]{1,0:T(8,128)S(1)}, f32[32,128]{1,0:T(8,128)S(1)}, u32[]{:S(2)}, u32[]{:S(2)}) collective-permute-start(f32[32,128]{1,0:T(8,128)S(1)} %get-tuple-element.34), channel_id=1, source_target_pairs={{0,7},{1,4},{2,5},{3,6},{4,3},{5,0},{6,1},{7,2},{8,15},{9,12},{10,... | collective-permute-start | bytes 49160 | tf_op jit(solution)/shard_map/ppermute | solution.py:37
  7.0 11.8 %collective-permute-start.4 = (f32[48,256]{1,0:T(8,128)S(1)}, f32[48,256]{1,0:T(8,128)S(1)}, u32[]{:S(2)}, u32[]{:S(2)}) collective-permute-start(f32[48,256]{1,0:T(8,128)S(1)} %get-tuple-element.39), channel_id=1, source_target_pairs={{0,3},{1,0},{2,1},{3,2},{4,7},{5,4},{6,5},{7,6},{8,11},{9,8},{10,9... | collective-permute-start | bytes 147464 | tf_op jit(solution)/shard_map/ppermute | solution.py:37
  7.6 11.3 %collective-permute-start.5 = (f32[48,256]{1,0:T(8,128)S(1)}, f32[48,256]{1,0:T(8,128)S(1)}, u32[]{:S(2)}, u32[]{:S(2)}) collective-permute-start(f32[48,256]{1,0:T(8,128)S(1)} %get-tuple-element.40), channel_id=1, source_target_pairs={{0,4},{4,0},{1,5},{5,1},{2,6},{6,2},{3,7},{7,3},{8,12},{12,8},{9,1... | collective-permute-start | bytes 147464 | tf_op jit(solution)/shard_map/ppermute | solution.py:37
  9.1 9.8 %collective-permute-start.6 = (f32[48,256]{1,0:T(8,128)S(1)}, f32[48,256]{1,0:T(8,128)S(1)}, u32[]{:S(2)}, u32[]{:S(2)}) collective-permute-start(f32[48,256]{1,0:T(8,128)S(1)} %get-tuple-element.41), channel_id=1, source_target_pairs={{0,24},{8,0},{16,8},{24,16},{1,25},{9,1},{17,9},{25,17},{2,26},{10... | collective-permute-start | bytes 147464 | tf_op jit(solution)/shard_map/ppermute | solution.py:37
  12.7 4.0 %collective-permute-start.3 = (f32[64,128]{1,0:T(8,128)S(1)}, f32[64,128]{1,0:T(8,128)S(1)}, u32[]{:S(2)}, u32[]{:S(2)}) collective-permute-start(f32[64,128]{1,0:T(8,128)S(1)} %shard_map.125), channel_id=1, source_target_pairs={{0,24},{8,0},{16,8},{24,16},{1,25},{9,1},{17,9},{25,17},{2,26},{10... | collective-permute-start | bytes 98312 | tf_op jit(solution)/shard_map/ppermute | solution.py:37
where the time goes:
time: 32.8 us; the launch traced here: 32.6 us
  blocking collectives  11.8 us (36%)
  starting transfers between devices  10.7 us (33%)
  Pallas kernels  7.42 us (23%)
  waiting for transfers between devices  1.93 us (6%)
  between operations  0.68 us (2%)
    all_to_all x1, blocking collectives, on_device(): received = lax.all_to_all(chunks, AXES, 0, 0, tiled=True)  11.8 us
    ppermute x7, starting transfers between devices, shifted(): return lax.ppermute(value, axes, pairs)  10.7 us
    pallas_call x7, Pallas kernels, call(): pl.pallas_call(kernel, out_shape=[jax.ShapeDtypeStruct(shape, dtype) for...  7.42 us
    ppermute x7, waiting for transfers between devices, shifted(): return lax.ppermute(value, axes, pairs)  1.93 us
  transfers between devices with their start and end apart: 7, of which 1 were waited for; matrix products, arithmetic and copies ran while one was open for 0% of the time, Pallas kernels for 11%

commit v1 on v0

--- a/solution.py
+++ b/solution.py
@@ -84,19 +84,39 @@
     return jnp.where((lane >= 2 * face) & (lane < 3 * face + edge), moved, send)
 
 
-def send_one_hot(send_row, first, rows):
-    row = iota((rows, send_row.shape[1]), 0) + first
-    return one_hot(row == send_row)
+def chosen_rows(blocks, low, high, parts):
+    rows = blocks[0].shape[0]
+    stacked = jnp.concatenate(split_parts(jnp.concatenate(blocks, axis=0), parts), axis=0)
+    found = join_parts(dot_nn(stacked, low), rows * len(blocks), parts)
+    high = jnp.broadcast_to(high, (rows, high.shape[1]))
+    total = None
+    for block in range(len(blocks)):
+        part = jnp.where(high == block, found[block * rows : (block + 1) * rows], 0.0)
+        total = part if total is None else total + part
+    return total
+
+
+def type_table(rep_ref, disp_ref, charge_ref):
+    sub = iota((8, rep_ref.shape[1]), 0)
+    rows = jnp.where(sub == 1, disp_ref[...], jnp.where(sub == 2, charge_ref[...], 0.0))
+    return jnp.where(sub == 0, rep_ref[...], rows)
+
+
+def row_one_hot(values, first, rows):
+    lanes = values.shape[1]
+    near = jnp.clip(values - first, -1, rows).astype(f32).astype(bf16)
+    column = iota((rows, 128), 0).astype(f32).astype(bf16)
+    column = jnp.concatenate([column] * (lanes // 128), axis=1)
+    return jnp.where(column == jnp.broadcast_to(near, (rows, lanes)), jnp.ones((), bf16), jnp.zeros((), bf16))
 
 
 def export_kernel(
     sizes,
     send_hbm, coords_hbm, types_hbm, rep_hbm, disp_hbm, charge_hbm, step_hbm, diff_hbm, anchor_hbm, neigh_hbm, live_hbm,
     pay_z_ref, pay_y_ref, pay_x_ref, pay_e_ref,
-    far_z_ref, far_y_ref, far_x_ref,
-    par_ref, order_ref,
-    coords_ref, step_ref, diff_ref, anchor_ref, neigh_ref, live_ref,
-    data_ref, send_pad_ref, send_ref, types_ref, rep_ref, disp_ref, charge_ref, arrived,
+    order_ref,
+    coords_ref, step_ref, diff_ref, anchor_ref, neigh_ref, live_ref, types_ref, rep_ref, disp_ref, charge_ref,
+    data_ref, send_pad_ref, send_ref, arrived,
 ):
     face, edge, _ = sizes
     faces, _ = slab_order(sizes)
@@ -119,29 +139,29 @@
         send_pad_ref[:, first : first + width] = send_ref[pl.ds(first, width)].reshape(1, width)
     send = reordered_send(send_pad_ref[:, : faces + 128], sizes)
     order_ref[:, : faces + 128] = send
-    kinds = one_hot(types_ref[...] == iota((ntypes, atoms), 0))
-    sub = iota((8, ntypes), 0)
-    table = jnp.where(sub == 0, rep_ref[...], jnp.where(sub == 1, disp_ref[...], jnp.where(sub == 2, charge_ref[...], 0.0)))
-    table = jnp.concatenate(split_parts(table, 3), axis=0)
-    params = join_parts(dot_nn(table, kinds), 8, 3)
-    par_ref[...] = params
+    high = send >> 7
+    low = row_one_hot(send & 127, 0, 128)
     data_ref[0:3, :] = coords_ref[...]
-    data_ref[3:6, :] = params[0:3]
-    data_ref[6:8, :] = params[6:8]
-    head = data_ref[...]
+    data_ref[3:4, :] = types_ref[...].astype(f32)
+    data_ref[4:8, :] = jnp.zeros((4, atoms), f32)
+    head = chosen_rows([data_ref[:, first : first + 128] for first in range(0, atoms, 128)], low, high, 3)
+    kinds = row_one_hot(head[3:4].astype(i32), 0, ntypes)
+    table = type_table(rep_ref, disp_ref, charge_ref)
+    params = join_parts(dot_nn(jnp.concatenate(split_parts(table, 3), axis=0), kinds), 8, 3)
+    head = jnp.where(iota(head.shape, 0) < 3, head, pltpu.roll(params, 3, 0))
     for copy in copies[6:]:
         copy.wait()
-    hist = jnp.concatenate([step_ref[...].reshape(-1, atoms), diff_ref[...].reshape(-1, atoms)], axis=0)
-    rows = hist.shape[0]
-    left = jnp.concatenate(split_parts(head, 3) + split_parts(hist, 2), axis=0)
-    total = None
-    chunk = 256
-    for first in range(0, atoms, chunk):
-        part = dot_nn(left[:, first : first + chunk], send_one_hot(send, first, chunk))
-        total = part if total is None else total + part
-    head = join_parts(total[0:24], 8, 3)
-    hist = join_parts(total[24:], rows, 2)
-    tail = jnp.concatenate([head[:, faces:], hist[:, faces:], jnp.zeros((8, 128), f32)], axis=0)
+    hist = jnp.concatenate(
+        [
+            chosen_rows(
+                [ref[c, :, first : first + 128] for first in range(0, atoms, 128)], low[:, faces:], high[:, faces:], 2
+            )
+            for ref in (step_ref, diff_ref)
+            for c in range(3)
+        ],
+        axis=0,
+    )
+    tail = jnp.concatenate([head[:, faces:], hist, jnp.zeros((8, 128), f32)], axis=0)
     packs = [packed_slab(tail, place, edge) for place in range(4)]
     for place, (ref, pack) in enumerate(((pay_z_ref, 1), (pay_y_ref, 2), (pay_x_ref, None))):
         ref[0:8, :] = head[:, place * face : place * face + 128]
@@ -150,8 +170,21 @@
             ref[16:32, :] = packs[pack]
     pay_e_ref[0:16, :] = packs[0]
     pay_e_ref[16:32, :] = packs[3]
+
+
+def history_kernel(step_ref, diff_ref, order_ref, far_z_ref, far_y_ref, far_x_ref):
+    atoms = step_ref.shape[2]
+    face = far_z_ref.shape[1]
+    hist = jnp.concatenate([step_ref[...].reshape(-1, atoms), diff_ref[...].reshape(-1, atoms)], axis=0)
+    left = jnp.concatenate(split_parts(hist, 2), axis=0)
+    total = None
+    chunk = 256
+    for first in range(0, atoms, chunk):
+        part = dot_nn(left[:, first : first + chunk], row_one_hot(order_ref[:, : 3 * face], first, chunk))
+        total = part if total is None else total + part
+    total = join_parts(total, hist.shape[0], 2)
     for place, ref in enumerate((far_z_ref, far_y_ref, far_x_ref)):
-        ref[...] = hist[:, place * face : (place + 1) * face]
+        ref[...] = total[:, place * face : (place + 1) * face]
 
 
 def packed_slab(tail, place, edge):
@@ -170,45 +203,57 @@
     )
 
 
-def cluster_map(atoms, clusters):
-    return one_hot((iota((atoms, clusters), 0) >> 3) == iota((atoms, clusters), 1))
-
-
-def to_clusters(rows6, lanes, clusters):
+def to_clusters(rows6, cluster_row, clusters):
+    lanes = rows6[0].shape[1]
     spread = spread_rows(rows6, lanes)
     left = jnp.concatenate(split_parts(spread, 3), axis=0)
-    return join_parts(dot_nn(left, cluster_map(lanes, clusters)), spread.shape[0], 3)
+    chosen = row_one_hot(cluster_row, 0, clusters)
+    return join_parts(dot_nt(left, chosen), spread.shape[0], 3)
 
 
 def to_atoms(tiles, lanes):
-    clusters = tiles.shape[1]
-    spread = one_hot((iota((clusters, lanes), 1) >> 3) == iota((clusters, lanes), 0))
-    wide = dot_nn(jnp.concatenate(split_parts(tiles, 3), axis=0), spread)
-    wide = join_parts(wide, tiles.shape[0], 3)
-    keep = (iota((8, lanes), 1) & 7) == iota((8, lanes), 0)
-    rows = []
-    for comp in range(tiles.shape[0] // 8):
-        slab = wide[comp * 8 : (comp + 1) * 8]
-        rows.append(jnp.sum(jnp.where(keep, slab, 0.0), axis=0, keepdims=True))
-    return rows
+    rows = tiles.shape[0]
+    blocks = lanes // 128
+    group = iota((rows, 128), 1) >> 4
+    picked = [
+        jnp.where(group == block % 8, tiles[:, block // 8 * 128 : block // 8 * 128 + 128], 0.0) for block in range(blocks)
+    ]
+    spread = one_hot((iota((128, 128), 0) & 15) == (iota((128, 128), 1) >> 3))
+    left = jnp.concatenate(split_parts(jnp.concatenate(picked, axis=0), 2), axis=0)
+    wide = join_parts(dot_nn(left, spread), rows * blocks, 2)
+    keep = (iota((8, 128), 1) & 7) == iota((8, 128), 0)
+    result = []
+    for comp in range(rows // 8):
+        pieces = []
+        for block in range(blocks):
+            first = block * rows + comp * 8
+            pieces.append(jnp.sum(jnp.where(keep, wide[first : first + 8], 0.0), axis=0, keepdims=True))
+        result.append(jnp.concatenate(pieces, axis=1))
+    return result
 
 
 def lane_sum(value):
     return jnp.sum(value, axis=1, keepdims=True)
 
 
-def local_kernel(coords_ref, par_ref, neigh_ref, tiles_ref, other_ref):
+def local_kernel(
+    coords_ref, types_ref, rep_ref, disp_ref, charge_ref, neigh_ref, tiles_ref, other_ref
+):
     atoms = coords_ref.shape[1]
     clusters = atoms // 8
     slots = neigh_ref.shape[0]
-    rows6 = [coords_ref[c : c + 1, :] for c in range(3)] + [par_ref[c : c + 1, :] for c in range(3)]
-    tiles = to_clusters(rows6, atoms, clusters)
+    table = type_table(rep_ref, disp_ref, charge_ref)
+    kinds = row_one_hot(types_ref[...], 0, table.shape[1])
+    params = join_parts(dot_nn(jnp.concatenate(split_parts(table, 3), axis=0), kinds), 8, 3)
+    rows6 = [coords_ref[c : c + 1, :] for c in range(3)] + [params[c : c + 1] for c in range(3)]
+    tiles = to_clusters(rows6, iota((1, atoms), 1) >> 3, clusters)
     tiles_ref[...] = tiles
     left = jnp.concatenate(split_parts(tiles, 3), axis=0)
     rows = tiles.shape[0]
     for slot in range(slots):
-        select = one_hot(iota((clusters, clusters), 0) == neigh_ref[slot : slot + 1, :])
-        other_ref[:, slot * clusters : (slot + 1) * clusters] = join_parts(dot_nn(left, select), rows, 3)
+        cols = slice(slot * clusters, (slot + 1) * clusters)
+        select = row_one_hot(neigh_ref[slot : slot + 1, :], 0, clusters)
+        other_ref[:, cols] = join_parts(dot_nn(left, select), rows, 3)
 
 
 def gram_kernel(step_ref, diff_ref, gram_ref):
@@ -260,11 +305,39 @@
     return code // 4, code // 2 % 2, code % 2
 
 
+def shifted_rows(rows, inside):
+    moved = [rows[c : c + 1] + jnp.where(inside[c], domain_side, 0.0) for c in range(3)]
+    return moved + [rows[c : c + 1] for c in range(3, 6)]
+
+
+def prep_kernel(sizes, other_ref, neigh_ref, pz_ref, py_ref, pe_ref, near_ref, select_ref, low_ref):
+    face, edge, _ = sizes
+    slots, clusters = neigh_ref.shape
+    faces, edges = slab_order(sizes)
+    halves = [ref[first : first + 8, :] for ref in (pz_ref, py_ref) for first in (0, 8)]
+    rows = jnp.concatenate(halves + [pe_ref[0:8, :]], axis=1)
+    lanes = rows.shape[1]
+    lane = iota((1, lanes), 1)
+    inside = (lane < 0, lane >= face, (lane < face) | (lane >= 2 * face))
+    used = lane < 2 * face + edge
+    rows6 = [jnp.where(used, row, 0.0) for row in shifted_rows(rows, inside)]
+    place = lane + jnp.where(lane < 2 * face, 0, face)
+    tiles = to_clusters(rows6, place >> 3, select_ref.shape[0])
+    left = jnp.concatenate(split_parts(tiles, 3), axis=0)
+    neigh = remapped(neigh_ref[...], clusters, sizes) - clusters
+    for slot in range(slots):
+        cols = slice(slot * clusters, (slot + 1) * clusters)
+        select = row_one_hot(neigh[slot : slot + 1, :], 0, select_ref.shape[0])
+        select_ref[:, cols] = select
+        low_ref[:, cols] = row_one_hot((neigh[slot : slot + 1, :] + clusters) & 127, 0, 128)
+        near_ref[:, cols] = other_ref[:, cols] + join_parts(dot_nn(left, select), tiles.shape[0], 3)
+
+
 def pair_kernel(
-    sizes, tiles_ref, other_ref, gram_ref, pz_ref, py_ref, px_ref, pe_ref, neigh_ref, live_ref,
-    coords_ref, anchor_ref, step_ref, diff_ref,
+    sizes, tiles_ref, near_ref, low_ref, halo_select_ref, gram_ref, px_ref,
+    neigh_ref, live_ref, coords_ref, anchor_ref, step_ref, diff_ref,
     grad_ref, returned_ref, common_ref,
-    select_ref, gather_ref, push_ref,
+    gather_ref, push_ref,
 ):
     face, edge, _ = sizes
     atoms = coords_ref.shape[1]
@@ -272,55 +345,42 @@
     slots = neigh_ref.shape[0]
     faces, edges = slab_order(sizes)
     lanes = faces + 128
-    halo_clusters = 128
     memory = step_ref.shape[1]
 
     group = iota((8, 128), 1) // edge
-    tail = jnp.where(
-        group == 0,
-        pe_ref[0:8, :],
-        jnp.where(
-            group == 1,
-            pltpu.roll(px_ref[16:24, :], edge, 1),
-            jnp.where(group == 2, pltpu.roll(px_ref[32:40, :], 2 * edge, 1), pltpu.roll(px_ref[48:56, :], 3 * edge, 1)),
-        ),
-    )
-    halves = [ref[first : first + 8, :] for ref in (pz_ref, py_ref, px_ref) for first in (0, 8)]
-    halo = jnp.concatenate(halves + [tail], axis=1)
-    lane = iota((1, lanes), 1)
-    in_x = (lane >= 2 * face) & ((lane < faces) | (lane >= faces + edge))
-    in_y = ((lane >= face) & (lane < 2 * face)) | ((lane >= faces) & (lane < faces + edge)) | (lane >= faces + 2 * edge)
-    in_z = (lane < face) | ((lane >= faces) & (lane < faces + 2 * edge)) | (lane >= faces + 3 * edge)
-    rows6 = [halo[c : c + 1] for c in range(6)]
-    for c, inside in enumerate((in_x, in_y, in_z)):
-        rows6[c] = rows6[c] + jnp.where(inside, domain_side, 0.0)
-    rows6 = [jnp.where(lane < faces + edges, row, 0.0) for row in rows6]
-    halo_tiles = to_clusters(rows6, lanes, halo_clusters)
-    left = jnp.concatenate(split_parts(halo_tiles, 3), axis=0)
-    rows = halo_tiles.shape[0]
-
-    neigh = remapped(neigh_ref[...], clusters, sizes)
+    tail = jnp.zeros((8, 128), f32)
+    for place in (1, 2, 3):
+        block = pltpu.roll(px_ref[16 * place : 16 * place + 8, :], place * edge, 1)
+        tail = jnp.where(group == place, block, tail)
+    rows = jnp.concatenate([px_ref[0:8, :], px_ref[8:16, :], tail], axis=1)
+    lane = iota((1, face + 128), 1)
+    inside = (lane >= 0, lane >= face + 2 * edge, ((lane >= face) & (lane < face + 2 * edge)) | (lane >= face + 3 * edge))
+    used = (lane < face) | ((lane >= face + edge) & (lane < face + edges))
+    rows6 = [jnp.where(used, row, 0.0) for row in shifted_rows(rows, inside)]
+    tiles = to_clusters(rows6, (lane + 2 * face) >> 3, halo_select_ref.shape[0])
+    left = jnp.concatenate(split_parts(tiles, 3), axis=0)
     for slot in range(slots):
         cols = slice(slot * clusters, (slot + 1) * clusters)
-        row = neigh[slot : slot + 1, :]
-        select_ref[:, cols] = one_hot(iota((clusters + halo_clusters, clusters), 0) == row)
-        far = dot_nn(left, select_ref[clusters:, cols])
-        gather_ref[:, cols] = other_ref[:, cols] + join_parts(far, rows, 3)
-
+        far = dot_nn(left, halo_select_ref[:, cols])
+        gather_ref[:, cols] = near_ref[:, cols] + join_parts(far, tiles.shape[0], 3)
+
+    neigh = neigh_ref[...]
     rank = iota((8, clusters), 0)
     home_id = iota((8, clusters), 1)
     live = jnp.broadcast_to(live_ref[...], (8, clusters))
     full = []
     half = []
     for slot in range(slots):
-        on = jnp.where(live > slot, 1.0, 0.0)
+        on = jnp.where(live > slot, 1.0, jnp.inf)
         full.append(on)
-        half.append(jnp.where(neigh[slot : slot + 1, :] == home_id, 0.0, on))
+        half.append(jnp.where(neigh[slot : slot + 1, :] == home_id, jnp.inf, on))
 
     energy = jnp.zeros((8, clusters), f32)
+    half_coulomb = jnp.zeros((8, clusters), f32)
     home_rows = [[None] * 8 for _ in range(3)]
     for p in range(8):
         home = [jnp.broadcast_to(tiles_ref[c * 8 + p : c * 8 + p + 1, :], (8, clusters)) for c in range(6)]
+        home[5] = 0.5 * home[5]
         upper = rank > p
         sums = [jnp.zeros((8, clusters), f32) for _ in range(3)]
         for slot in range(slots):
@@ -328,14 +388,14 @@
             other = [gather_ref[c * 8 : (c + 1) * 8, cols] for c in range(6)]
             offset = [home[c] - other[c] for c in range(3)]
             dist_sq = offset[0] * offset[0] + offset[1] * offset[1] + offset[2] * offset[2]
-            root = lax.rsqrt(1.0 + dist_sq)
+            root = lax.rsqrt(dist_sq + jnp.where(upper, full[slot], half[slot]))
             inverse = root * root
             repulse = home[3] * other[3] * inverse
-            attract = home[4] * other[4]
+            less = repulse - home[4] * other[4]
             coulomb = home[5] * other[5] * root
-            weight = jnp.where(upper, full[slot], half[slot])
-            energy = energy + weight * (inverse * (repulse - attract) + coulomb)
-            factor = weight * inverse * (inverse * (4.0 * repulse - 2.0 * attract) + coulomb)
+            energy = energy + inverse * less
+            half_coulomb = half_coulomb + coulomb
+            factor = inverse * (inverse * (repulse + less) + coulomb)
             for c in range(3):
                 term = factor * offset[c]
                 sums[c] = sums[c] + term
@@ -343,11 +403,18 @@
                 push_ref[place] = term if p == 0 else push_ref[place] + term
         for c in range(3):
             home_rows[c][p] = jnp.sum(sums[c], axis=0, keepdims=True)
+    energy = energy + 2.0 * half_coulomb
     home_grad = jnp.concatenate([home_rows[c][p] for c in range(3) for p in range(8)], axis=0)
     back = jnp.concatenate(split_parts(push_ref[...], 2), axis=0)
-    tile_grad = join_parts(dot_nt(back, select_ref[...]), 24, 2)
-    own = to_atoms(tile_grad[:, :clusters] - home_grad, atoms)
-    returned = to_atoms(tile_grad[:, clusters:], lanes)
+    high = remapped(neigh, clusters, sizes) >> 7
+    high = jnp.concatenate([high[slot : slot + 1] for slot in range(slots)], axis=1).astype(f32).astype(bf16)
+    high = jnp.broadcast_to(high, back.shape)
+    held = clusters // 128 + 1
+    masked = [jnp.where(high == jnp.array(block, bf16), back, jnp.zeros((), bf16)) for block in range(held)]
+    tile_grad = dot_nt(jnp.concatenate(masked, axis=0), low_ref[...])
+    tile_grad = [join_parts(tile_grad[48 * block : 48 * block + 48], 24, 2) for block in range(held)]
+    own = to_atoms(2.0 * (jnp.concatenate(tile_grad[:-1], axis=1) - home_grad), atoms)
+    returned = to_atoms(2.0 * tile_grad[-1], lanes)
 
     step_dots = jnp.zeros((memory, atoms), f32)
     diff_dots = jnp.zeros((memory, atoms), f32)
@@ -423,7 +490,7 @@
         chunk_ref[target, 0 : 3 * len(pieces), :] = jnp.concatenate(pieces, axis=0)
 
 
-def finish_kernel(sizes, atoms_total, recv_ref, send_ref, grad_ref, coords_ref, step_ref, diff_ref, new_ref, energy_ref):
+def finish_kernel(sizes, atoms_total, recv_ref, order_ref, grad_ref, coords_ref, step_ref, diff_ref, new_ref, energy_ref):
     _, edge, _ = sizes
     faces, edges = slab_order(sizes)
     atoms = coords_ref.shape[1]
@@ -481,17 +548,20 @@
     for code in (1, 2, 4):
         pieces += [blocks[code][0:3], blocks[code][3:6]]
     pieces.append(tail[0:3])
-    returned = jnp.concatenate([jnp.concatenate(pieces, axis=1), jnp.zeros((5, faces + 128), f32)], axis=0)
-    back = jnp.concatenate(split_parts(returned, 2), axis=0)
-    send = send_ref[:, : faces + 128]
-    added = []
-    chunk = 256
-    for first in range(0, atoms, chunk):
-        added.append(join_parts(dot_nt(back, send_one_hot(send, first, chunk)), 8, 2))
-    added = jnp.concatenate(added, axis=1)
+    returned = jnp.concatenate(pieces, axis=1)
+    send = order_ref[:, : faces + 128]
+    blocks = atoms // 128
+    high = jnp.broadcast_to(send >> 7, (blocks, faces + 128)) == iota((blocks, faces + 128), 0)
+    spread = [jnp.where(high, jnp.broadcast_to(returned[c : c + 1], high.shape), 0.0) for c in range(3)]
+    back = jnp.concatenate(split_parts(jnp.concatenate(spread, axis=0), 2), axis=0)
+    tiles = join_parts(dot_nt(back, row_one_hot(send & 127, 0, 128)), 3 * blocks, 2)
+    added = [
+        jnp.concatenate([tiles[c * blocks + block : c * blocks + block + 1] for block in range(blocks)], axis=1)
+        for c in range(3)
+    ]
     widen = atoms // 128
     for c in range(3):
-        grad = grad_ref[c : c + 1, :] + added[c : c + 1, :]
+        grad = grad_ref[c : c + 1, :] + added[c]
         mixed = jnp.tile(coef, (1, widen)) * step_ref[c] + jnp.tile(diff_coef, (1, widen)) * diff_ref[c]
         direction = jnp.tile(scaling[0:1], (1, widen)) * grad + jnp.sum(mixed, axis=0, keepdims=True)
         new_ref[c : c + 1, :] = coords_ref[c : c + 1, :] - step_length * direction
@@ -540,31 +610,26 @@
     live = live_counts[None]
     rows = 6 * memory
 
-    ntypes = rep_coef.shape[0]
-    pay_z, pay_y, pay_x, pay_e, far_z, far_y, far_x, params, order, coords_v, steps_v, diffs_v, anchor_v, neigh_v, live_v = call(
+    types, tables = atom_types[None], [table[None] for table in (rep_coef, disp_coef, charge)]
+    pay_z, pay_y, pay_x, pay_e, order, coords_v, steps_v, diffs_v, anchor_v, neigh_v, live_v, *types_v = call(
         functools.partial(export_kernel, sizes),
         [((32, 128), f32)] * 2
-        + [((16, 128), f32), ((32, 128), f32)]
-        + [((rows, face), f32)] * 3
-        + [((8, atoms), f32), ((1, wide), i32)]
-        + [(value.shape, value.dtype) for value in (coords, steps, diffs, anchor, neigh, live)],
+        + [((16, 128), f32), ((32, 128), f32), ((1, wide), i32)]
+        + [(value.shape, value.dtype) for value in (coords, steps, diffs, anchor, neigh, live, types, *tables)],
         [
             pltpu.VMEM((8, atoms), f32),
             pltpu.VMEM((1, wide), i32),
             pltpu.VMEM(halo_send.shape, i32),
-            pltpu.VMEM((1, atoms), i32),
-            pltpu.VMEM((1, ntypes), f32),
-            pltpu.VMEM((1, ntypes), f32),
-            pltpu.VMEM((1, ntypes), f32),
             pltpu.SemaphoreType.DMA((11,)),
         ],
-        halo_send, coords, atom_types[None], rep_coef[None], disp_coef[None], charge[None],
+        halo_send, coords, types, *tables,
         steps, diffs, anchor, neigh, live,
         space=pltpu.HBM,
     )
     pe = shifted(pay_e, ("gy", "gz"), -1)
     py = shifted(pay_y, ("gy",), -1)
     pz = shifted(pay_z, ("gz",), -1)
+    far_z, far_y, far_x = call(history_kernel, [((rows, face), f32)] * 3, [], steps_v, diffs_v, order)
     fx = shifted(far_x, ("gx",), -1)
     fy = shifted(far_y, ("gy",), -1)
     fz = shifted(far_z, ("gz",), -1)
@@ -572,21 +637,23 @@
         local_kernel,
         [((48, clusters), f32), ((48, slots * clusters), f32)],
         [],
-        coords_v, params, neigh_v,
+        coords_v, *types_v, neigh_v,
     )
     (pay_x,) = call(merge_kernel, [((64, 128), f32)], [], pay_x, pz, py, pe, limit_mib=4)
     px = shifted(pay_x, ("gx",), -1)
+    near, halo_select, low_select = call(
+        functools.partial(prep_kernel, sizes),
+        [((48, slots * clusters), f32)] + [((128, slots * clusters), bf16)] * 2,
+        [],
+        other, neigh_v, pz, py, pe,
+    )
     (gram,) = call(gram_kernel, [((memory, 128), f32)], [], steps_v, diffs_v, limit_mib=8)
     grad, returned, common = call(
         functools.partial(pair_kernel, sizes),
         [((3, atoms), f32), ((3, lanes), f32), ((8, 128), f32)],
-        [
-            pltpu.VMEM((clusters + 128, slots * clusters), bf16),
-            pltpu.VMEM((48, slots * clusters), f32),
-            pltpu.VMEM((24, slots * clusters), f32),
-        ],
-        tiles, other, gram, pz, py, px, pe, neigh_v, live_v, coords_v, anchor_v, steps_v, diffs_v,
-        limit_mib=24,
+        [pltpu.VMEM((48, slots * clusters), f32), pltpu.VMEM((24, slots * clusters), f32)],
+        tiles, near, low_select, halo_select, gram, px, neigh_v, live_v, coords_v, anchor_v, steps_v, diffs_v,
+        limit_mib=16,
     )
     (chunks,) = call(
         functools.partial(chunk_kernel, sizes),

time: 32.8 us -> 31.5 us (0.960)
  waiting for transfers between devices: 1.93 us -> 1.36 us
    ppermute x7, waiting for transfers between devices: 1.93 us -> 1.36 us  [shifted(): return lax.ppermute(value, axes, pairs)]
    all_to_all x1, blocking collectives: 11.8 us -> 11.5 us  [on_device(): received = lax.all_to_all(chunks, AXES, 0, 0, tiled=True)]
    pallas_call x7 -> x9, Pallas kernels: 7.42 us -> 7.31 us  [call(): pl.pallas_call(kernel, out_shape=[jax.ShapeDtypeStruct(shape, dtype) for...]
  transfers between devices with their start and end apart: 7 -> 7, of which waited for: 1 -> 1; matrix products, arithmetic and copies ran while one was open for 0% -> 0% of each run, Pallas kernels for 11% -> 14%
where the time goes in v1:
time: 31.5 us; the launch traced here: 31.3 us
  blocking collectives  11.5 us (37%)
  starting transfers between devices  10.5 us (33%)
  Pallas kernels  7.31 us (23%)
  waiting for transfers between devices  1.36 us (4%)
  between operations  0.7 us (2%)
    all_to_all x1, blocking collectives, on_device(): received = lax.all_to_all(chunks, AXES, 0, 0, tiled=True)  11.5 us
    ppermute x7, starting transfers between devices, shifted(): return lax.ppermute(value, axes, pairs)  10.5 us
    pallas_call x9, Pallas kernels, call(): pl.pallas_call(kernel, out_shape=[jax.ShapeDtypeStruct(shape, dtype) for...  7.31 us
    ppermute x7, waiting for transfers between devices, shifted(): return lax.ppermute(value, axes, pairs)  1.36 us
  transfers between devices with their start and end apart: 7, of which 1 were waited for; matrix products, arithmetic and copies ran while one was open for 0% of the time, Pallas kernels for 14%

profile of v1, /device:TPU:0, one launch (start us, length us, event | category | flops | bytes accessed | tf_op | source)
XLA Modules:
  0.0 31.3 jit_solution(670559749546968092)
XLA Ops:
  0.6 1.8 %shard_map.122 = (f32[32,128]{1,0:T(8,128)S(1)}, f32[32,128]{1,0:T(8,128)S(1)}, f32[16,128]{1,0:T(8,128)S(1)}, f32[32,128]{1,0:T(8,128)S(1)}, s32[1,1024]{1,0:T(...) custom-call(s32[872]{0:T(1024)} %send_hbm.1, ...), custom_call_target="tpu_custom_call" | custom-call | tf_op jit(solution)/shard_map/pallas_call | solution.py:573
  2.4 2.5 %collective-permute-start = (f32[32,128]{1,0:T(8,128)S(1)}, f32[32,128]{1,0:T(8,128)S(1)}, u32[]{:S(2)}, u32[]{:S(2)}) collective-permute-start(f32[32,128]{1,0:T(8,128)S(1)} %get-tuple-element.38), channel_id=1, source_target_pairs={{0,3},{1,0},{2,1},{3,2},{4,7},{5,4},{6,5},{7,6},{8,11},{9,8},{10,9... | collective-permute-start | bytes 49160 | tf_op jit(solution)/shard_map/ppermute | solution.py:37
  4.9 1.5 %collective-permute-start.1 = (f32[32,128]{1,0:T(8,128)S(1)}, f32[32,128]{1,0:T(8,128)S(1)}, u32[]{:S(2)}, u32[]{:S(2)}) collective-permute-start(f32[32,128]{1,0:T(8,128)S(1)} %get-tuple-element.39), channel_id=1, source_target_pairs={{0,4},{4,0},{1,5},{5,1},{2,6},{6,2},{3,7},{7,3},{8,12},{12,8},{9,1... | collective-permute-start | bytes 49160 | tf_op jit(solution)/shard_map/ppermute | solution.py:37
  6.4 0.3 %collective-permute-start.2 = (f32[32,128]{1,0:T(8,128)S(1)}, f32[32,128]{1,0:T(8,128)S(1)}, u32[]{:S(2)}, u32[]{:S(2)}) collective-permute-start(f32[32,128]{1,0:T(8,128)S(1)} %get-tuple-element.40), channel_id=1, source_target_pairs={{0,7},{1,4},{2,5},{3,6},{4,3},{5,0},{6,1},{7,2},{8,15},{9,12},{10,... | collective-permute-start | bytes 49160 | tf_op jit(solution)/shard_map/ppermute | solution.py:37
  6.8 0.6 %shard_map.128 = (f32[48,256]{1,0:T(8,128)S(1)}, f32[48,256]{1,0:T(8,128)S(1)}, f32[48,256]{1,0:T(8,128)S(1)}) custom-call(f32[3,8,2048]{2,1,0:T(8,128)S(1)} %get-tuple-element.44.step_ref, f32[3,8,2048]{2,1,0:T(8,128)S(1)} %get-tuple-element.45.diff_ref, s32[1,1024]{1,0:T(1,128)S(1)} %get-tuple-element.51.order_ref), custom_call_target="tpu_custom_call" | custom-call | tf_op jit(solution)/shard_map/pallas_call | solution.py:573
  7.4 0.6 %collective-permute-start.4 = (f32[48,256]{1,0:T(8,128)S(1)}, f32[48,256]{1,0:T(8,128)S(1)}, u32[]{:S(2)}, u32[]{:S(2)}) collective-permute-start(f32[48,256]{1,0:T(8,128)S(1)} %get-tuple-element.52), channel_id=1, source_target_pairs={{0,3},{1,0},{2,1},{3,2},{4,7},{5,4},{6,5},{7,6},{8,11},{9,8},{10,9... | collective-permute-start | bytes 147464 | tf_op jit(solution)/shard_map/ppermute | solution.py:37
  8.0 1.5 %collective-permute-start.5 = (f32[48,256]{1,0:T(8,128)S(1)}, f32[48,256]{1,0:T(8,128)S(1)}, u32[]{:S(2)}, u32[]{:S(2)}) collective-permute-start(f32[48,256]{1,0:T(8,128)S(1)} %get-tuple-element.53), channel_id=1, source_target_pairs={{0,4},{4,0},{1,5},{5,1},{2,6},{6,2},{3,7},{7,3},{8,12},{12,8},{9,1... | collective-permute-start | bytes 147464 | tf_op jit(solution)/shard_map/ppermute | solution.py:37
  9.5 0.0 collective-permute-done.pz_ref
  9.5 3.6 %collective-permute-start.6 = (f32[48,256]{1,0:T(8,128)S(1)}, f32[48,256]{1,0:T(8,128)S(1)}, u32[]{:S(2)}, u32[]{:S(2)}) collective-permute-start(f32[48,256]{1,0:T(8,128)S(1)} %get-tuple-element.54), channel_id=1, source_target_pairs={{0,24},{8,0},{16,8},{24,16},{1,25},{9,1},{17,9},{25,17},{2,26},{10... | collective-permute-start | bytes 147464 | tf_op jit(solution)/shard_map/ppermute | solution.py:37
  13.1 0.0 collective-permute-done.1.py_ref
  13.1 0.0 collective-permute-done.2.pe_ref
  13.1 0.5 %collective-permute-start.3 = (f32[64,128]{1,0:T(8,128)S(1)}, f32[64,128]{1,0:T(8,128)S(1)}, u32[]{:S(2)}, u32[]{:S(2)}) collective-permute-start(f32[64,128]{1,0:T(8,128)S(1)} %shard_map.126), channel_id=1, source_target_pairs={{0,24},{8,0},{16,8},{24,16},{1,25},{9,1},{17,9},{25,17},{2,26},{10... | collective-permute-start | bytes 98312 | tf_op jit(solution)/shard_map/ppermute | solution.py:37
  13.6 0.4 %shard_map.125.gram_ref = f32[8,128]{1,0:T(8,128)S(1)} custom-call(f32[3,8,2048]{2,1,0:T(8,128)S(1)} %get-tuple-element.44.step_ref, f32[3,8,2048]{2,1,0:T(8,128)S(1)} %get-tuple-element.45.diff_ref), custom_call_target="tpu_custom_call" | custom-call | tf_op jit(solution)/shard_map/pallas_call | solution.py:573
  14.0 1.1 %shard_map.123 = (f32[48,256]{1,0:T(8,128)S(1)}, f32[48,2048]{1,0:T(8,128)S(1)}) custom-call(f32[3,2048]{1,0:T(4,128)S(1)} %get-tuple-element.30.coords_ref, s32[1,2048]{1,0:T(1,128)S(1)} %get-tuple-element.31.types_ref, f32[1,64]{1,0:T(1,128)S(1)} %get-tuple-element.32.rep_ref, f32[1,64]{1,0:T(1,128)S(1)} %get-tuple-element.33.disp_ref, ...), custom_call_target="tpu_custom_call" | custom-call | tf_op jit(solution)/shard_map/pallas_call | solution.py:573
  15.1 0.6 %shard_map.124 = (f32[48,2048]{1,0:T(8,128)S(1)}, bf16[128,2048]{1,0:T(8,128)(2,1)S(1)}, bf16[128,2048]{1,0:T(8,128)(2,1)S(1)}) custom-call(f32[48,2048]{1,0:T(8,128)S(1)} %get-tuple-element.37.other_ref, s32[8,256]{1,0:T(8,128)S(1)} %get-tuple-element.35.neigh_ref, f32[32,128]{1,0:T(8,128)S(1)} %collective-permute-done.pz_ref, ...), custom_call_target="tpu_custom_call" | custom-call | tf_op jit(solution)/shard_map/pallas_call | solution.py:573
  15.8 1.3 %collective-permute-done.3.px_ref = f32[64,128]{1,0:T(8,128)S(1)} collective-permute-done((f32[64,128]{1,0:T(8,128)S(1)}, f32[64,128]{1,0:T(8,128)S(1)}, u32[]{:S(2)}, u32[]{:S(2)}) %collective-permute-start.3) | collective-permute-done | bytes 32800 | tf_op jit(solution)/shard_map/ppermute | solution.py:37
  17.1 1.6 %shard_map.127 = (f32[3,2048]{1,0:T(4,128)S(1)}, f32[3,896]{1,0:T(4,128)S(1)}, f32[8,128]{1,0:T(8,128)S(1)}) custom-call(f32[48,256]{1,0:T(8,128)S(1)} %get-tuple-element.36.tiles_ref, f32[48,2048]{1,0:T(8,128)S(1)} %get-tuple-element.41.near_ref, bf16[128,2048]{1,0:T(8,128)(2,1)S(1)} %get-tuple-element.42.low_ref, ...), custom_call_target="tpu_custom_call" | custom-call | tf_op jit(solution)/shard_map/pallas_call | solution.py:573
  18.7 0.0 collective-permute-done.4.fz_ref
  18.7 0.0 collective-permute-done.5.fy_ref
  18.7 0.0 collective-permute-done.6.fx_ref
  18.7 0.2 shard_map.129
  18.9 11.5 %all_to_all.5.recv_ref = f32[32,8,128]{2,1,0:T(8,128)S(1)} all-to-all(f32[32,8,128]{2,1,0:T(8,128)S(1)} %shard_map.129), channel_id=1, replica_groups=mesh['gx'=4,'gy'=2,'gz'=4] {'gx','gy','gz'}, dimensions={0} | all-to-all | bytes 262144 | tf_op jit(solution)/shard_map/all_to_all | solution.py:665
  30.4 0.9 %shard_map.130 = (f32[3,2048]{1,0:T(4,128)}, f32[1,1]{1,0:T(1,128)}) custom-call(f32[32,8,128]{2,1,0:T(8,128)S(1)} %all_to_all.5.recv_ref, s32[1,1024]{1,0:T(1,128)S(1)} %get-tuple-element.51.order_ref, f32[3,2048]{1,0:T(4,128)S(1)} %get-tuple-element.55.grad_ref, f32[3,2048]{1,0:T(4,128)S(1)} %get-tuple-element.30.coords_ref, ...), custom_call_target="tpu_custom_call" | custom-call | tf_op jit(solution)/shard_map/pallas_call | solution.py:573
  (1 shorter events, 0.0 us)
Async XLA Ops:
  2.4 7.1 %collective-permute-start = (f32[32,128]{1,0:T(8,128)S(1)}, f32[32,128]{1,0:T(8,128)S(1)}, u32[]{:S(2)}, u32[]{:S(2)}) collective-permute-start(f32[32,128]{1,0:T(8,128)S(1)} %get-tuple-element.38), channel_id=1, source_target_pairs={{0,3},{1,0},{2,1},{3,2},{4,7},{5,4},{6,5},{7,6},{8,11},{9,8},{10,9... | collective-permute-start | bytes 49160 | tf_op jit(solution)/shard_map/ppermute | solution.py:37
  4.9 8.2 %collective-permute-start.1 = (f32[32,128]{1,0:T(8,128)S(1)}, f32[32,128]{1,0:T(8,128)S(1)}, u32[]{:S(2)}, u32[]{:S(2)}) collective-permute-start(f32[32,128]{1,0:T(8,128)S(1)} %get-tuple-element.39), channel_id=1, source_target_pairs={{0,4},{4,0},{1,5},{5,1},{2,6},{6,2},{3,7},{7,3},{8,12},{12,8},{9,1... | collective-permute-start | bytes 49160 | tf_op jit(solution)/shard_map/ppermute | solution.py:37
  6.4 6.7 %collective-permute-start.2 = (f32[32,128]{1,0:T(8,128)S(1)}, f32[32,128]{1,0:T(8,128)S(1)}, u32[]{:S(2)}, u32[]{:S(2)}) collective-permute-start(f32[32,128]{1,0:T(8,128)S(1)} %get-tuple-element.40), channel_id=1, source_target_pairs={{0,7},{1,4},{2,5},{3,6},{4,3},{5,0},{6,1},{7,2},{8,15},{9,12},{10,... | collective-permute-start | bytes 49160 | tf_op jit(solution)/shard_map/ppermute | solution.py:37
  7.4 11.3 %collective-permute-start.4 = (f32[48,256]{1,0:T(8,128)S(1)}, f32[48,256]{1,0:T(8,128)S(1)}, u32[]{:S(2)}, u32[]{:S(2)}) collective-permute-start(f32[48,256]{1,0:T(8,128)S(1)} %get-tuple-element.52), channel_id=1, source_target_pairs={{0,3},{1,0},{2,1},{3,2},{4,7},{5,4},{6,5},{7,6},{8,11},{9,8},{10,9... | collective-permute-start | bytes 147464 | tf_op jit(solution)/shard_map/ppermute | solution.py:37
  8.0 10.7 %collective-permute-start.5 = (f32[48,256]{1,0:T(8,128)S(1)}, f32[48,256]{1,0:T(8,128)S(1)}, u32[]{:S(2)}, u32[]{:S(2)}) collective-permute-start(f32[48,256]{1,0:T(8,128)S(1)} %get-tuple-element.53), channel_id=1, source_target_pairs={{0,4},{4,0},{1,5},{5,1},{2,6},{6,2},{3,7},{7,3},{8,12},{12,8},{9,1... | collective-permute-start | bytes 147464 | tf_op jit(solution)/shard_map/ppermute | solution.py:37
  9.5 9.2 %collective-permute-start.6 = (f32[48,256]{1,0:T(8,128)S(1)}, f32[48,256]{1,0:T(8,128)S(1)}, u32[]{:S(2)}, u32[]{:S(2)}) collective-permute-start(f32[48,256]{1,0:T(8,128)S(1)} %get-tuple-element.54), channel_id=1, source_target_pairs={{0,24},{8,0},{16,8},{24,16},{1,25},{9,1},{17,9},{25,17},{2,26},{10... | collective-permute-start | bytes 147464 | tf_op jit(solution)/shard_map/ppermute | solution.py:37
  13.1 4.0 %collective-permute-start.3 = (f32[64,128]{1,0:T(8,128)S(1)}, f32[64,128]{1,0:T(8,128)S(1)}, u32[]{:S(2)}, u32[]{:S(2)}) collective-permute-start(f32[64,128]{1,0:T(8,128)S(1)} %shard_map.126), channel_id=1, source_target_pairs={{0,24},{8,0},{16,8},{24,16},{1,25},{9,1},{17,9},{25,17},{2,26},{10... | collective-permute-start | bytes 98312 | tf_op jit(solution)/shard_map/ppermute | solution.py:37

commit v2 on v1

--- a/solution.py
+++ b/solution.py
@@ -275,11 +275,14 @@
     gram_ref[...] = placed
 
 
-def merge_kernel(pay_ref, pz_ref, py_ref, pe_ref, out_ref):
+def merge_kernel(edge, pay_ref, pz_ref, py_ref, pe_ref, out_ref, rest_ref):
     out_ref[0:16, :] = pay_ref[...]
-    out_ref[16:32, :] = pz_ref[16:32, :]
-    out_ref[32:48, :] = py_ref[16:32, :]
-    out_ref[48:64, :] = pe_ref[16:32, :]
+    group = iota((8, 128), 1) // edge
+    tail = jnp.zeros((8, 128), f32)
+    for place, ref in ((1, pz_ref), (2, py_ref), (3, pe_ref)):
+        tail = jnp.where(group == place, pltpu.roll(ref[16:24, :], place * edge, 1), tail)
+        rest_ref[16 * place - 16 : 16 * place, :] = ref[16:32, :]
+    out_ref[16:24, :] = tail
 
 
 def remapped(neigh, clusters, sizes):
@@ -347,12 +350,7 @@
     lanes = faces + 128
     memory = step_ref.shape[1]
 
-    group = iota((8, 128), 1) // edge
-    tail = jnp.zeros((8, 128), f32)
-    for place in (1, 2, 3):
-        block = pltpu.roll(px_ref[16 * place : 16 * place + 8, :], place * edge, 1)
-        tail = jnp.where(group == place, block, tail)
-    rows = jnp.concatenate([px_ref[0:8, :], px_ref[8:16, :], tail], axis=1)
+    rows = jnp.concatenate([px_ref[first : first + 8, :] for first in (0, 8, 16)], axis=1)
     lane = iota((1, face + 128), 1)
     inside = (lane >= 0, lane >= face + 2 * edge, ((lane >= face) & (lane < face + 2 * edge)) | (lane >= face + 3 * edge))
     used = (lane < face) | ((lane >= face + edge) & (lane < face + edges))
@@ -446,7 +444,7 @@
     return jnp.sum(dots, axis=0, keepdims=True)
 
 
-def chunk_kernel(sizes, common_ref, returned_ref, fz_ref, fy_ref, fx_ref, px_ref, pe_ref, chunk_ref):
+def chunk_kernel(sizes, common_ref, returned_ref, fz_ref, fy_ref, fx_ref, fe_ref, pe_ref, chunk_ref):
     face, edge, _ = sizes
     faces, _ = slab_order(sizes)
     rows = fy_ref.shape[0]
@@ -463,7 +461,7 @@
     group = iota((1, 128), 1) // edge
     above_sum = jnp.zeros((memory, 128), f32)
     below_sum = jnp.zeros((memory, 128), f32)
-    packs = (pe_ref[0:16, :], px_ref[16:32, :], px_ref[32:48, :], px_ref[48:64, :])
+    packs = (pe_ref[0:16, :], fe_ref[0:16, :], fe_ref[16:32, :], fe_ref[32:48, :])
     tails = jnp.concatenate([returned[:, faces:], jnp.zeros((5, 128), f32)], axis=0)
     for place, pack in enumerate(packs):
         turned = [pltpu.roll(tails, (k - place) % 4 * edge, 1) for k in range(4)]
@@ -639,8 +637,15 @@
         [],
         coords_v, *types_v, neigh_v,
     )
-    (pay_x,) = call(merge_kernel, [((64, 128), f32)], [], pay_x, pz, py, pe, limit_mib=4)
+    pay_x, far_e = call(
+        functools.partial(merge_kernel, edge),
+        [((24, 128), f32), ((48, 128), f32)],
+        [],
+        pay_x, pz, py, pe,
+        limit_mib=4,
+    )
     px = shifted(pay_x, ("gx",), -1)
+    fe = shifted(far_e, ("gx",), -1)
     near, halo_select, low_select = call(
         functools.partial(prep_kernel, sizes),
         [((48, slots * clusters), f32)] + [((128, slots * clusters), bf16)] * 2,
@@ -659,7 +664,7 @@
         functools.partial(chunk_kernel, sizes),
         [((devices, 8, 128), f32)],
         [],
-        common, returned, fz, fy, fx, px, pe,
+        common, returned, fz, fy, fx, fe, pe,
         limit_mib=24,
     )
     received = lax.all_to_all(chunks, AXES, 0, 0, tiled=True)

time: 31.5 us -> 33.9 us (1.076)
  waiting for transfers between devices: 1.36 us -> 4.46 us
  starting transfers between devices: 10.5 us -> 9.9 us
    ppermute x7 -> x8, waiting for transfers between devices: 1.36 us -> 4.46 us  [shifted(): return lax.ppermute(value, axes, pairs)]
    ppermute x7 -> x8, starting transfers between devices: 10.5 us -> 9.9 us  [shifted(): return lax.ppermute(value, axes, pairs)]
  transfers between devices with their start and end apart: 7 -> 8, of which waited for: 1 -> 2; matrix products, arithmetic and copies ran while one was open for 0% -> 0% of each run, Pallas kernels for 14% -> 13%
where the time goes in v2:
time: 33.9 us; the launch traced here: 33.7 us
  blocking collectives  11.2 us (33%)
  starting transfers between devices  9.9 us (29%)
  Pallas kernels  7.39 us (22%)
  waiting for transfers between devices  4.46 us (13%)
  between operations  0.71 us (2%)
    all_to_all x1, blocking collectives, on_device(): received = lax.all_to_all(chunks, AXES, 0, 0, tiled=True)  11.2 us
    ppermute x8, starting transfers between devices, shifted(): return lax.ppermute(value, axes, pairs)  9.9 us
    pallas_call x9, Pallas kernels, call(): pl.pallas_call(kernel, out_shape=[jax.ShapeDtypeStruct(shape, dtype) for...  7.39 us
    ppermute x8, waiting for transfers between devices, shifted(): return lax.ppermute(value, axes, pairs)  4.46 us
  transfers between devices with their start and end apart: 8, of which 2 were waited for; matrix products, arithmetic and copies ran while one was open for 0% of the time, Pallas kernels for 13%

profile of v2, /device:TPU:0, one launch (start us, length us, event | category | flops | bytes accessed | tf_op | source)
XLA Modules:
  0.0 33.7 jit_solution(8311638361419654720)
XLA Ops:
  0.6 1.8 %shard_map.122 = (f32[32,128]{1,0:T(8,128)S(1)}, f32[32,128]{1,0:T(8,128)S(1)}, f32[16,128]{1,0:T(8,128)S(1)}, f32[32,128]{1,0:T(8,128)S(1)}, s32[1,1024]{1,0:T(...) custom-call(s32[872]{0:T(1024)} %send_hbm.1, ...), custom_call_target="tpu_custom_call" | custom-call | tf_op jit(solution)/shard_map/pallas_call | solution.py:571
  2.4 2.5 %collective-permute-start = (f32[32,128]{1,0:T(8,128)S(1)}, f32[32,128]{1,0:T(8,128)S(1)}, u32[]{:S(2)}, u32[]{:S(2)}) collective-permute-start(f32[32,128]{1,0:T(8,128)S(1)} %get-tuple-element.40), channel_id=1, source_target_pairs={{0,3},{1,0},{2,1},{3,2},{4,7},{5,4},{6,5},{7,6},{8,11},{9,8},{10,9... | collective-permute-start | bytes 49160 | tf_op jit(solution)/shard_map/ppermute | solution.py:37
  4.9 0.6 %shard_map.128 = (f32[48,256]{1,0:T(8,128)S(1)}, f32[48,256]{1,0:T(8,128)S(1)}, f32[48,256]{1,0:T(8,128)S(1)}) custom-call(f32[3,8,2048]{2,1,0:T(8,128)S(1)} %get-tuple-element.46.step_ref, f32[3,8,2048]{2,1,0:T(8,128)S(1)} %get-tuple-element.47.diff_ref, s32[1,1024]{1,0:T(1,128)S(1)} %get-tuple-element.54.order_ref), custom_call_target="tpu_custom_call" | custom-call | tf_op jit(solution)/shard_map/pallas_call | solution.py:571
  5.5 0.7 %collective-permute-start.4 = (f32[48,256]{1,0:T(8,128)S(1)}, f32[48,256]{1,0:T(8,128)S(1)}, u32[]{:S(2)}, u32[]{:S(2)}) collective-permute-start(f32[48,256]{1,0:T(8,128)S(1)} %get-tuple-element.55), channel_id=1, source_target_pairs={{0,3},{1,0},{2,1},{3,2},{4,7},{5,4},{6,5},{7,6},{8,11},{9,8},{10,9... | collective-permute-start | bytes 147464 | tf_op jit(solution)/shard_map/ppermute | solution.py:37
  6.3 1.5 %collective-permute-start.5 = (f32[48,256]{1,0:T(8,128)S(1)}, f32[48,256]{1,0:T(8,128)S(1)}, u32[]{:S(2)}, u32[]{:S(2)}) collective-permute-start(f32[48,256]{1,0:T(8,128)S(1)} %get-tuple-element.56), channel_id=1, source_target_pairs={{0,4},{4,0},{1,5},{5,1},{2,6},{6,2},{3,7},{7,3},{8,12},{12,8},{9,1... | collective-permute-start | bytes 147464 | tf_op jit(solution)/shard_map/ppermute | solution.py:37
  7.8 3.6 %collective-permute-start.6 = (f32[48,256]{1,0:T(8,128)S(1)}, f32[48,256]{1,0:T(8,128)S(1)}, u32[]{:S(2)}, u32[]{:S(2)}) collective-permute-start(f32[48,256]{1,0:T(8,128)S(1)} %get-tuple-element.57), channel_id=1, source_target_pairs={{0,24},{8,0},{16,8},{24,16},{1,25},{9,1},{17,9},{25,17},{2,26},{10... | collective-permute-start | bytes 147464 | tf_op jit(solution)/shard_map/ppermute | solution.py:37
  11.4 0.5 %collective-permute-start.1 = (f32[32,128]{1,0:T(8,128)S(1)}, f32[32,128]{1,0:T(8,128)S(1)}, u32[]{:S(2)}, u32[]{:S(2)}) collective-permute-start(f32[32,128]{1,0:T(8,128)S(1)} %get-tuple-element.41), channel_id=1, source_target_pairs={{0,4},{4,0},{1,5},{5,1},{2,6},{6,2},{3,7},{7,3},{8,12},{12,8},{9,1... | collective-permute-start | bytes 49160 | tf_op jit(solution)/shard_map/ppermute | solution.py:37
  11.9 0.0 collective-permute-done.pz_ref
  11.9 0.2 collective-permute-start.2
  12.1 3.3 %collective-permute-done.1.py_ref = f32[32,128]{1,0:T(8,128)S(1)} collective-permute-done((f32[32,128]{1,0:T(8,128)S(1)}, f32[32,128]{1,0:T(8,128)S(1)}, u32[]{:S(2)}, u32[]{:S(2)}) %collective-permute-start.1) | collective-permute-done | bytes 16416 | tf_op jit(solution)/shard_map/ppermute | solution.py:37
  15.4 0.0 collective-permute-done.2.pe_ref
  15.4 0.1 shard_map.126
  15.5 0.5 %collective-permute-start.7 = (f32[48,128]{1,0:T(8,128)S(1)}, f32[48,128]{1,0:T(8,128)S(1)}, u32[]{:S(2)}, u32[]{:S(2)}) collective-permute-start(f32[48,128]{1,0:T(8,128)S(1)} %get-tuple-element.58), channel_id=1, source_target_pairs={{0,24},{8,0},{16,8},{24,16},{1,25},{9,1},{17,9},{25,17},{2,26},{10... | collective-permute-start | bytes 73736 | tf_op jit(solution)/shard_map/ppermute | solution.py:37
  16.0 0.4 %collective-permute-start.3 = (f32[24,128]{1,0:T(8,128)S(1)}, f32[24,128]{1,0:T(8,128)S(1)}, u32[]{:S(2)}, u32[]{:S(2)}) collective-permute-start(f32[24,128]{1,0:T(8,128)S(1)} %get-tuple-element.49), channel_id=1, source_target_pairs={{0,24},{8,0},{16,8},{24,16},{1,25},{9,1},{17,9},{25,17},{2,26},{10... | collective-permute-start | bytes 36872 | tf_op jit(solution)/shard_map/ppermute | solution.py:37
  16.4 0.4 %shard_map.125.gram_ref = f32[8,128]{1,0:T(8,128)S(1)} custom-call(f32[3,8,2048]{2,1,0:T(8,128)S(1)} %get-tuple-element.46.step_ref, f32[3,8,2048]{2,1,0:T(8,128)S(1)} %get-tuple-element.47.diff_ref), custom_call_target="tpu_custom_call" | custom-call | tf_op jit(solution)/shard_map/pallas_call | solution.py:571
  16.8 1.1 %shard_map.123 = (f32[48,256]{1,0:T(8,128)S(1)}, f32[48,2048]{1,0:T(8,128)S(1)}) custom-call(f32[3,2048]{1,0:T(4,128)S(1)} %get-tuple-element.32.coords_ref, s32[1,2048]{1,0:T(1,128)S(1)} %get-tuple-element.33.types_ref, f32[1,64]{1,0:T(1,128)S(1)} %get-tuple-element.34.rep_ref, f32[1,64]{1,0:T(1,128)S(1)} %get-tuple-element.35.disp_ref, ...), custom_call_target="tpu_custom_call" | custom-call | tf_op jit(solution)/shard_map/pallas_call | solution.py:571
  17.9 0.6 %shard_map.124 = (f32[48,2048]{1,0:T(8,128)S(1)}, bf16[128,2048]{1,0:T(8,128)(2,1)S(1)}, bf16[128,2048]{1,0:T(8,128)(2,1)S(1)}) custom-call(f32[48,2048]{1,0:T(8,128)S(1)} %get-tuple-element.39.other_ref, s32[8,256]{1,0:T(8,128)S(1)} %get-tuple-element.37.neigh_ref, f32[32,128]{1,0:T(8,128)S(1)} %collective-permute-done.pz_ref, ...), custom_call_target="tpu_custom_call" | custom-call | tf_op jit(solution)/shard_map/pallas_call | solution.py:571
  18.5 1.1 %collective-permute-done.3.px_ref = f32[24,128]{1,0:T(8,128)S(1)} collective-permute-done((f32[24,128]{1,0:T(8,128)S(1)}, f32[24,128]{1,0:T(8,128)S(1)}, u32[]{:S(2)}, u32[]{:S(2)}) %collective-permute-start.3) | collective-permute-done | bytes 12320 | tf_op jit(solution)/shard_map/ppermute | solution.py:37
  19.7 1.6 %shard_map.127 = (f32[3,2048]{1,0:T(4,128)S(1)}, f32[3,896]{1,0:T(4,128)S(1)}, f32[8,128]{1,0:T(8,128)S(1)}) custom-call(f32[48,256]{1,0:T(8,128)S(1)} %get-tuple-element.38.tiles_ref, f32[48,2048]{1,0:T(8,128)S(1)} %get-tuple-element.43.near_ref, bf16[128,2048]{1,0:T(8,128)(2,1)S(1)} %get-tuple-element.44.low_ref, ...), custom_call_target="tpu_custom_call" | custom-call | tf_op jit(solution)/shard_map/pallas_call | solution.py:571
  21.3 0.0 collective-permute-done.7.fe_ref
  21.3 0.0 collective-permute-done.4.fz_ref
  21.3 0.0 collective-permute-done.5.fy_ref
  21.3 0.0 collective-permute-done.6.fx_ref
  21.3 0.2 shard_map.129
  21.5 11.2 %all_to_all.5.recv_ref = f32[32,8,128]{2,1,0:T(8,128)S(1)} all-to-all(f32[32,8,128]{2,1,0:T(8,128)S(1)} %shard_map.129), channel_id=1, replica_groups=mesh['gx'=4,'gy'=2,'gz'=4] {'gx','gy','gz'}, dimensions={0} | all-to-all | bytes 262144 | tf_op jit(solution)/shard_map/all_to_all | solution.py:670
  32.7 0.9 %shard_map.130 = (f32[3,2048]{1,0:T(4,128)}, f32[1,1]{1,0:T(1,128)}) custom-call(f32[32,8,128]{2,1,0:T(8,128)S(1)} %all_to_all.5.recv_ref, s32[1,1024]{1,0:T(1,128)S(1)} %get-tuple-element.54.order_ref, f32[3,2048]{1,0:T(4,128)S(1)} %get-tuple-element.59.grad_ref, f32[3,2048]{1,0:T(4,128)S(1)} %get-tuple-element.32.coords_ref, ...), custom_call_target="tpu_custom_call" | custom-call | tf_op jit(solution)/shard_map/pallas_call | solution.py:571
Async XLA Ops:
  2.4 9.5 %collective-permute-start = (f32[32,128]{1,0:T(8,128)S(1)}, f32[32,128]{1,0:T(8,128)S(1)}, u32[]{:S(2)}, u32[]{:S(2)}) collective-permute-start(f32[32,128]{1,0:T(8,128)S(1)} %get-tuple-element.40), channel_id=1, source_target_pairs={{0,3},{1,0},{2,1},{3,2},{4,7},{5,4},{6,5},{7,6},{8,11},{9,8},{10,9... | collective-permute-start | bytes 49160 | tf_op jit(solution)/shard_map/ppermute | solution.py:37
  5.5 15.8 %collective-permute-start.4 = (f32[48,256]{1,0:T(8,128)S(1)}, f32[48,256]{1,0:T(8,128)S(1)}, u32[]{:S(2)}, u32[]{:S(2)}) collective-permute-start(f32[48,256]{1,0:T(8,128)S(1)} %get-tuple-element.55), channel_id=1, source_target_pairs={{0,3},{1,0},{2,1},{3,2},{4,7},{5,4},{6,5},{7,6},{8,11},{9,8},{10,9... | collective-permute-start | bytes 147464 | tf_op jit(solution)/shard_map/ppermute | solution.py:37
  6.3 15.0 %collective-permute-start.5 = (f32[48,256]{1,0:T(8,128)S(1)}, f32[48,256]{1,0:T(8,128)S(1)}, u32[]{:S(2)}, u32[]{:S(2)}) collective-permute-start(f32[48,256]{1,0:T(8,128)S(1)} %get-tuple-element.56), channel_id=1, source_target_pairs={{0,4},{4,0},{1,5},{5,1},{2,6},{6,2},{3,7},{7,3},{8,12},{12,8},{9,1... | collective-permute-start | bytes 147464 | tf_op jit(solution)/shard_map/ppermute | solution.py:37
  7.8 13.5 %collective-permute-start.6 = (f32[48,256]{1,0:T(8,128)S(1)}, f32[48,256]{1,0:T(8,128)S(1)}, u32[]{:S(2)}, u32[]{:S(2)}) collective-permute-start(f32[48,256]{1,0:T(8,128)S(1)} %get-tuple-element.57), channel_id=1, source_target_pairs={{0,24},{8,0},{16,8},{24,16},{1,25},{9,1},{17,9},{25,17},{2,26},{10... | collective-permute-start | bytes 147464 | tf_op jit(solution)/shard_map/ppermute | solution.py:37
  11.4 4.0 %collective-permute-start.1 = (f32[32,128]{1,0:T(8,128)S(1)}, f32[32,128]{1,0:T(8,128)S(1)}, u32[]{:S(2)}, u32[]{:S(2)}) collective-permute-start(f32[32,128]{1,0:T(8,128)S(1)} %get-tuple-element.41), channel_id=1, source_target_pairs={{0,4},{4,0},{1,5},{5,1},{2,6},{6,2},{3,7},{7,3},{8,12},{12,8},{9,1... | collective-permute-start | bytes 49160 | tf_op jit(solution)/shard_map/ppermute | solution.py:37
  11.9 3.5 %collective-permute-start.2 = (f32[32,128]{1,0:T(8,128)S(1)}, f32[32,128]{1,0:T(8,128)S(1)}, u32[]{:S(2)}, u32[]{:S(2)}) collective-permute-start(f32[32,128]{1,0:T(8,128)S(1)} %get-tuple-element.42), channel_id=1, source_target_pairs={{0,7},{1,4},{2,5},{3,6},{4,3},{5,0},{6,1},{7,2},{8,15},{9,12},{10,... | collective-permute-start | bytes 49160 | tf_op jit(solution)/shard_map/ppermute | solution.py:37
  15.5 5.8 %collective-permute-start.7 = (f32[48,128]{1,0:T(8,128)S(1)}, f32[48,128]{1,0:T(8,128)S(1)}, u32[]{:S(2)}, u32[]{:S(2)}) collective-permute-start(f32[48,128]{1,0:T(8,128)S(1)} %get-tuple-element.58), channel_id=1, source_target_pairs={{0,24},{8,0},{16,8},{24,16},{1,25},{9,1},{17,9},{25,17},{2,26},{10... | collective-permute-start | bytes 73736 | tf_op jit(solution)/shard_map/ppermute | solution.py:37
  16.0 3.7 %collective-permute-start.3 = (f32[24,128]{1,0:T(8,128)S(1)}, f32[24,128]{1,0:T(8,128)S(1)}, u32[]{:S(2)}, u32[]{:S(2)}) collective-permute-start(f32[24,128]{1,0:T(8,128)S(1)} %get-tuple-element.49), channel_id=1, source_target_pairs={{0,24},{8,0},{16,8},{24,16},{1,25},{9,1},{17,9},{25,17},{2,26},{10... | collective-permute-start | bytes 36872 | tf_op jit(solution)/shard_map/ppermute | solution.py:37
